TPU v7x, 128 devices: a whole 4x4x4 slice. The times are simulated.
128 devices in a mesh: dev: 128 (over y, z, x, core).
Axes of the slice: x: 4, y: 4, z: 4, core: 2. Of those that a mesh axis runs over, the one named last changes fastest.
Arguments:
- energies: bfloat16 [256, 2097152], P(None, 'dev'), may hold values from -270 to 12
- block_live_samples: int32 [4096], P('dev'), may hold values from 0 to 512, as said below
- block_owner: int32 [4096], P('dev'), may hold values from 0 to 127, as said below
- block_slot: int32 [4096], P('dev'), may hold values from 0 to 15
- state_counts: int32 [256], replicated, may hold values from 1000 to 60000
- start_free: float32 [256], replicated, may hold values from -6 to 6
Outputs:
- free_energy: float32 [256], replicated
- log_denominator: float32 [2048, 512], P('dev')
Inputs may be any that keep to these rules, and one draw needn't show every extreme that they name: `block_owner`: blocks with block_live_samples 0 hold no samples; their owner and slot are unused. Live blocks come in any slots of a device. Every device owns at most 16 live blocks, no two in the same owned slot, and some device owns exactly 16. A device sends at most one block to any other device, and some device does send one. `block_live_samples`: some devices hold up to 32 live blocks.
All inputs are finite; a program needn't handle non-finite values.
Results may differ from a plain program's by a relative error of at most 0.0003.
Values may be sent and summed in bfloat16 or wider, within the bound.
No kernel may reach another device: no remote copies, remote signals or barrier semaphores. Data moves between devices by JAX's collectives and lax.ppermute only.
A program may use at most 64 MiB of HBM per device.

v0:
```python
import jax
import jax.numpy as jnp
from jax import lax
from jax.sharding import Mesh
from jax.sharding import PartitionSpec as P

ITERS = 2
DEV = ("dev_0", "dev_1", "dev_2", "dev_3")


def copy_for_each(value, axis):
    size = lax.axis_size(axis)
    return lax.all_to_all(
        jnp.broadcast_to(value[None], (size, *value.shape)), axis, 0, 0, tiled=True
    )


def over_copies(value, axis):
    return copy_for_each(value, axis).sum(axis=0)


def over_axes(value, axes):
    far, near = axes
    return over_copies(over_copies(value, near), far)


def block_pass(blocks, live, offsets):
    shifted = offsets[:, None, None] - blocks.astype(jnp.float32)
    largest = jnp.max(shifted, axis=0)
    log_denom = largest + jnp.log(jnp.sum(jnp.exp(shifted - largest[None]), axis=0))
    log_denom = jnp.where(live, log_denom, jnp.zeros_like(log_denom))
    weights = jnp.where(live[None], jnp.exp(shifted - log_denom[None]), jnp.zeros_like(shifted))
    return (log_denom, jnp.sum(weights, axis=(1, 2)))


def iterate(blocks, live, state_counts, start_free):
    log_counts = jnp.log(state_counts.astype(jnp.float32))
    free_energy = start_free
    log_denom = jnp.zeros(live.shape, jnp.float32)
    for rounds in range(ITERS):
        offsets = log_counts + free_energy
        log_denom, partial_value = block_pass(blocks, live, offsets)
        total = over_axes(partial_value, (("dev_0", "dev_1", "dev_2"), "dev_3"))
        updated = offsets - jnp.log(total)
        free_energy = updated - updated[0]
    return (free_energy, log_denom)


def body(energies, block_live_samples, block_owner, block_slot, state_counts, start_free):
    myself = lax.axis_index(DEV)
    members = lax.axis_size(DEV)
    thermo_states, block_width = energies.shape
    slot_total = block_live_samples.shape[0]
    sample_extent = block_width // slot_total
    slot_capacity = slot_total // 2
    resident_blocks = energies.reshape(thermo_states, slot_total, sample_extent)
    peers = jnp.arange(members, dtype=jnp.int32)
    slot_identifiers = jnp.arange(slot_total, dtype=jnp.int32)
    holder = jnp.arange(slot_capacity, dtype=jnp.int32)
    moving = (block_live_samples > 0) & (block_owner != myself)
    staying = (block_live_samples > 0) & (block_owner == myself)
    matches = moving[None, :] & (block_owner[None, :] == peers[:, None])
    present = jnp.any(matches, axis=1)
    source = jnp.sum(jnp.where(matches, slot_identifiers[None, :], 0), axis=1)
    staying_here = staying[None, :] & (block_slot[None, :] == holder[:, None])
    from_home = jnp.any(staying_here, axis=1)
    home_index = jnp.sum(jnp.where(staying_here, slot_identifiers[None, :], 0), axis=1)
    lane_position_index = lax.broadcasted_iota(jnp.int32, (slot_total, sample_extent), 1)
    live = lane_position_index < block_live_samples[:, None]
    free_energy, log_denom = iterate(resident_blocks, live, state_counts, start_free)
    outgoing = jnp.where(present[:, None], jnp.take(log_denom, source, axis=0), 0.0)
    out_slot = jnp.where(present, block_slot[source], -1)[:, None]
    arrived, got_slot = (
        lax.all_to_all(outgoing, DEV, split_axis=0, concat_axis=0, tiled=True),
        lax.all_to_all(out_slot, DEV, split_axis=0, concat_axis=0, tiled=True),
    )
    got_slot = got_slot[:, 0]
    landed = got_slot[None, :] == holder[:, None]
    from_peer = jnp.any(landed, axis=1)
    peer_index = jnp.sum(jnp.where(landed, peers[None, :], 0), axis=1)
    home_rows = jnp.where(from_home[:, None], jnp.take(log_denom, home_index, axis=0), 0.0)
    placed = jnp.where(from_peer[:, None], jnp.take(arrived, peer_index, axis=0), home_rows)
    return (free_energy, placed)


def solution(mesh):
    split = Mesh(mesh.devices.reshape(4, 4, 4, 2), ("dev_0", "dev_1", "dev_2", "dev_3"))
    return jax.shard_map(
        body,
        mesh=split,
        in_specs=(P(None, DEV), P(DEV), P(DEV), P(DEV), P(), P()),
        out_specs=(P(), P(DEV, None)),
        check_vma=False,
    )
```

profile of v0, /device:TPU:1, one launch (start us, length us, event | category | flops | bytes accessed | tf_op | source)
XLA Modules:
  0.0 113.5 jit_solution(7251105366266459831)
XLA Ops:
  0.7 0.9 fusion.23
  1.5 5.9 %fusion.2 = f32[16384]{0:T(1024)S(1)} fusion(bf16[256,16384]{1,0:T(8,128)(2,1)} %param.6, f32[256]{0:T(256)S(1)} %fusion.23), kind=kLoop, calls=%fused_computation.8 | loop fusion | flops 12566528 | bytes 8455168 | tf_op jit(solution)/shard_map/reduce_max | solution.py:29
  7.4 3.4 %fusion.12 = f32[16384]{0:T(1024)S(1)} fusion(bf16[256,16384]{1,0:T(8,128)(2,1)S(1)} %copy-done.1, f32[16384]{0:T(1024)S(1)} %fusion.2, f32[256]{0:T(256)S(1)} %fusion.23), kind=kLoop, calls=%fused_computation.18 | loop fusion | flops 16760832 | bytes 8520704 | tf_op jit(solution)/shard_map/reduce_sum | solution.py:30
  11.0 4.9 %fusion.15 = f32[256]{0:T(256)S(1)} fusion(bf16[256,16384]{1,0:T(8,128)(2,1)S(1)} %copy-done.1, f32[16384]{0:T(1024)S(1)} %get-tuple-element.4, f32[256]{0:T(256)S(1)} %fusion.23, pred[16384]{0:T(1024)(128)(4,1)S(1)} %get-tuple-element.5), kind=kLoop, calls=%fused_computation.21 | loop fusion | flops 20971264 | bytes 8472576 | tf_op jit(solution)/shard_map/reduce_sum | solution.py:33
  15.9 0.6 broadcast_in_dim.160
  16.5 4.6 %all-to-all-start = ((f32[2,1,256]{2,1,0:T(1,128)}), f32[2,1,256]{2,1,0:T(1,128)S(1)}, u32[]{:S(2)}, u32[]{:S(2)}) async-start(f32[2,1,256]{2,1,0:T(1,128)} %broadcast_in_dim.160), calls=%async_computation | async-start | bytes 4096 | tf_op jit(solution)/shard_map/all_to_all | solution.py:13
  21.6 1.2 %gather_fusion = s32[128]{0:T(128)S(1)} fusion(s32[32]{0:T(128)S(1)} %copy-done, s32[1024]{0:T(1024)S(1)} %pad_clamp_fusion.2), kind=kCustom, calls=%fused_computation | custom fusion | bytes 1536 | tf_op jit(solution)/shard_map/gather | solution.py:72
  22.8 0.7 copy.18
  23.6 10.2 %all-to-all-start.4 = ((s32[128,1,1]{2,1,0:T(1,128)}), s32[128,1,1]{2,1,0:T(1,128)S(1)}, u32[]{:S(2)}, u32[]{:S(2)}) async-start(s32[128,1,1]{2,1,0:T(1,128)} %copy.18), calls=%async_computation.4 | async-start | bytes 131072 | tf_op jit(solution)/shard_map/all_to_all | solution.py:75
  33.8 9.5 %all-to-all-done.4 = s32[128,1,1]{2,1,0:T(1,128)S(1)} async-done(((s32[128,1,1]{2,1,0:T(1,128)}), s32[128,1,1]{2,1,0:T(1,128)S(1)}, u32[]{:S(2)}, u32[]{:S(2)}) %all-to-all-start.4) | async-done | bytes 544 | tf_op jit(solution)/shard_map/all_to_all | solution.py:75
  43.3 0.7 broadcast_in_dim.161
  44.0 4.9 %all-to-all-start.1 = ((f32[64,1,256]{2,1,0:T(1,128)}), f32[64,1,256]{2,1,0:T(1,128)S(1)}, u32[]{:S(2)}, u32[]{:S(2)}) async-start(f32[64,1,256]{2,1,0:T(1,128)} %broadcast_in_dim.161), calls=%async_computation.1 | async-start | bytes 131072 | tf_op jit(solution)/shard_map/all_to_all | solution.py:13
  48.8 2.4 %reduce.10 = s32[128]{0:T(128)S(1)} reduce(s32[128,1,1]{2,1,0:T(1,128)S(1)} %all-to-all-done.4, s32[]{:T(128)} %constant.33.clone.1), dimensions={1,2}, to_apply=%all_to_all.30.reduce_sub_computation | reduce | bytes 1028 | tf_op jit(solution)/shard_map/all_to_all | solution.py:75
  51.5 5.6 %all-to-all-done.1 = f32[64,1,256]{2,1,0:T(1,128)S(1)} async-done(((f32[64,1,256]{2,1,0:T(1,128)}), f32[64,1,256]{2,1,0:T(1,128)S(1)}, u32[]{:S(2)}, u32[]{:S(2)}) %all-to-all-start.1) | async-done | bytes 65568 | tf_op jit(solution)/shard_map/all_to_all | solution.py:13
  57.2 0.5 slice.6
  57.7 0.7 subtract_add_fusion
  58.4 5.6 %fusion.5 = f32[16384]{0:T(1024)S(1)} fusion(bf16[256,16384]{1,0:T(8,128)(2,1)} %param.6, f32[256]{0:T(256)S(1)} %subtract_add_fusion), kind=kLoop, calls=%fused_computation.11 | loop fusion | flops 12566528 | bytes 8455168 | tf_op jit(solution)/shard_map/reduce_max | solution.py:29
  64.0 7.0 %fusion.7 = f32[16384]{0:T(1024)S(1)} fusion(bf16[256,16384]{1,0:T(8,128)(2,1)} %param.6, f32[16384]{0:T(1024)S(1)} %fusion.5, f32[256]{0:T(256)S(1)} %subtract_add_fusion), kind=kLoop, calls=%fused_computation.13 | loop fusion | flops 16760832 | bytes 8520704 | tf_op jit(solution)/shard_map/reduce_sum | solution.py:30
  71.1 5.1 %fusion.10 = f32[256]{0:T(256)S(1)} fusion(bf16[256,16384]{1,0:T(8,128)(2,1)S(1)} %bitcast.28, f32[16384]{0:T(1024)S(1)} %get-tuple-element.2, f32[256]{0:T(256)S(1)} %subtract_add_fusion, pred[16384]{0:T(1024)(128)(4,1)S(1)} %get-tuple-element.5), kind=kLoop, calls=%fused_computation.16 | loop fusion | flops 20971264 | bytes 8472576 | tf_op jit(solution)/shard_map/reduce_sum | solution.py:33
  76.2 5.8 %all_to_all.39 = f32[2,1,256]{2,1,0:T(1,128)S(1)} all-to-all(f32[2,1,256]{2,1,0:T(1,128)S(1)} %broadcast_in_dim.162), channel_id=1, replica_groups=mesh['dev_0'=4,'dev_1'=4,'dev_2'=4,'dev_3'=2] {'dev_3'}, dimensions={0} | all-to-all | bytes 4096 | tf_op jit(solution)/shard_map/all_to_all | solution.py:13
  82.0 0.7 broadcast_in_dim.163
  82.7 4.7 %all-to-all-start.3 = ((f32[64,1,256]{2,1,0:T(1,128)}), f32[64,1,256]{2,1,0:T(1,128)S(1)}, u32[]{:S(2)}, u32[]{:S(2)}) async-start(f32[64,1,256]{2,1,0:T(1,128)} %broadcast_in_dim.163), calls=%async_computation.3 | async-start | bytes 131072 | tf_op jit(solution)/shard_map/all_to_all | solution.py:13
  87.5 0.8 gather_fusion.1
  88.3 0.6 gather_fusion.3
  88.9 1.0 copy.19
  89.9 5.9 %all-to-all-done.3 = f32[64,1,256]{2,1,0:T(1,128)S(1)} async-done(((f32[64,1,256]{2,1,0:T(1,128)}), f32[64,1,256]{2,1,0:T(1,128)S(1)}, u32[]{:S(2)}, u32[]{:S(2)}) %all-to-all-start.3) | async-done | bytes 65568 | tf_op jit(solution)/shard_map/all_to_all | solution.py:13
  95.8 5.3 %all-to-all-start.5 = ((f32[128,1,512]{2,1,0:T(1,128)}), f32[128,1,512]{2,1,0:T(1,128)S(1)}, u32[]{:S(2)}, u32[]{:S(2)}) async-start(f32[128,1,512]{2,1,0:T(1,128)} %copy.19), calls=%async_computation.5 | async-start | bytes 524288 | tf_op jit(solution)/shard_map/all_to_all | solution.py:74
  101.2 0.5 slice.7
  101.8 1.2 %broadcast_subtract_fusion = f32[256]{0:T(256)} fusion(f32[256]{0:T(256)S(1)} %log_subtract_fusion, f32[]{:T(128)} %bitcast.2), kind=kLoop, calls=%fused_computation.66 | loop fusion | flops 256 | bytes 2052 | tf_op jit(solution)/shard_map/sub | solution.py:45
  103.0 9.2 %all-to-all-done.5 = f32[128,1,512]{2,1,0:T(1,128)S(1)} async-done(((f32[128,1,512]{2,1,0:T(1,128)}), f32[128,1,512]{2,1,0:T(1,128)S(1)}, u32[]{:S(2)}, u32[]{:S(2)}) %all-to-all-start.5) | async-done | bytes 262176 | tf_op jit(solution)/shard_map/all_to_all | solution.py:74
  112.2 0.6 gather_fusion.2
  112.8 0.7 select_select_fusion
  (49 shorter events, 1.4 us)
Async XLA Ops:
  0.6 6.8 %copy-start.1 = (bf16[256,16384]{1,0:T(8,128)(2,1)S(1)}, bf16[256,16384]{1,0:T(8,128)(2,1)}, u32[]{:S(2)}) copy-start(bf16[256,16384]{1,0:T(8,128)(2,1)} %param.6) | copy-start | bytes 25165828
  1.5 9.4 %copy-start.2 = (s32[32]{0:T(128)S(1)}, s32[32]{0:T(128)}, u32[]{:S(2)}) copy-start(s32[32]{0:T(128)} %param.7) | copy-start | bytes 388
  7.4 13.7 %copy-start.4 = (s32[32]{0:T(128)S(1)}, s32[32]{0:T(128)}, u32[]{:S(2)}) copy-start(s32[32]{0:T(128)} %param.8) | copy-start | bytes 388
  7.4 13.9 %copy-start = (s32[32]{0:T(128)S(1)}, s32[32]{0:T(128)}, u32[]{:S(2)}) copy-start(s32[32]{0:T(128)} %param.9) | copy-start | bytes 388
  7.4 50.3 %copy-start.3 = (s32[256]{0:T(256)S(1)}, s32[256]{0:T(256)}, u32[]{:S(2)}) copy-start(s32[256]{0:T(256)} %param.10) | copy-start | bytes 3076
  16.5 7.1 %all-to-all-start = ((f32[2,1,256]{2,1,0:T(1,128)}), f32[2,1,256]{2,1,0:T(1,128)S(1)}, u32[]{:S(2)}, u32[]{:S(2)}) async-start(f32[2,1,256]{2,1,0:T(1,128)} %broadcast_in_dim.160), calls=%async_computation | async-start | bytes 4096 | tf_op jit(solution)/shard_map/all_to_all | solution.py:13
  23.6 19.8 %all-to-all-start.4 = ((s32[128,1,1]{2,1,0:T(1,128)}), s32[128,1,1]{2,1,0:T(1,128)S(1)}, u32[]{:S(2)}, u32[]{:S(2)}) async-start(s32[128,1,1]{2,1,0:T(1,128)} %copy.18), calls=%async_computation.4 | async-start | bytes 131072 | tf_op jit(solution)/shard_map/all_to_all | solution.py:75
  44.0 13.1 %all-to-all-start.1 = ((f32[64,1,256]{2,1,0:T(1,128)}), f32[64,1,256]{2,1,0:T(1,128)S(1)}, u32[]{:S(2)}, u32[]{:S(2)}) async-start(f32[64,1,256]{2,1,0:T(1,128)} %broadcast_in_dim.161), calls=%async_computation.1 | async-start | bytes 131072 | tf_op jit(solution)/shard_map/all_to_all | solution.py:13
  58.4 12.7 %slice-start = ((s8[8388608]{0:T(1024)(128)(4,1)}), s8[4194304]{0:T(1024)(128)(4,1)S(1)}, s32[]{:S(2)}) async-start(s8[8388608]{0:T(1024)(128)(4,1)} %bitcast.27), calls=%async_computation.6 | async-start | bytes 8388608
  64.0 7.0 %slice-start.1 = ((s8[8388608]{0:T(1024)(128)(4,1)}), s8[4194304]{0:T(1024)(128)(4,1)S(1)}, s32[]{:S(2)}) async-start(s8[8388608]{0:T(1024)(128)(4,1)} %bitcast.27), calls=%async_computation.7 | async-start | bytes 8388608
  82.7 13.1 %all-to-all-start.3 = ((f32[64,1,256]{2,1,0:T(1,128)}), f32[64,1,256]{2,1,0:T(1,128)S(1)}, u32[]{:S(2)}, u32[]{:S(2)}) async-start(f32[64,1,256]{2,1,0:T(1,128)} %broadcast_in_dim.163), calls=%async_computation.3 | async-start | bytes 131072 | tf_op jit(solution)/shard_map/all_to_all | solution.py:13
  95.8 16.4 %all-to-all-start.5 = ((f32[128,1,512]{2,1,0:T(1,128)}), f32[128,1,512]{2,1,0:T(1,128)S(1)}, u32[]{:S(2)}, u32[]{:S(2)}) async-start(f32[128,1,512]{2,1,0:T(1,128)} %copy.19), calls=%async_computation.5 | async-start | bytes 524288 | tf_op jit(solution)/shard_map/all_to_all | solution.py:74
where the time goes:
time: 114 us; the launch traced here: 113 us
  other arithmetic  38.8 us (34%)
  waiting for transfers between devices  30.3 us (27%)
  starting transfers between devices  29.7 us (26%)
  local copies, waits for them, and re-layouts  7.96 us (7%)
  blocking collectives  5.84 us (5%)
    all_to_all x3, starting transfers between devices, copy_for_each(): lax.all_to_all(jnp.broadcast_to(value[None], (size, *value.shape)), axis,...  14.1 us
    all_to_all x3, waiting for transfers between devices, copy_for_each(): lax.all_to_all(jnp.broadcast_to(value[None], (size, *value.shape)), axis,...  11.6 us
    reduce_max x2, other arithmetic, block_pass(): largest = jnp.max(shifted, axis=0)  11.5 us
    reduce_sum x2, other arithmetic, block_pass(): jnp.sum(jnp.exp(shifted - largest[None]), axis=0)  10.4 us
    all_to_all x1, starting transfers between devices, body(): lax.all_to_all(out_slot, DEV, split_axis=0, concat_axis=0, tiled=True)  10.2 us
    reduce_sum x2, other arithmetic, block_pass(): return (log_denom, jnp.sum(weights, axis=(1, 2)))  9.97 us
    all_to_all x1, waiting for transfers between devices, body(): lax.all_to_all(out_slot, DEV, split_axis=0, concat_axis=0, tiled=True)  9.49 us
    all_to_all x1, waiting for transfers between devices, body(): lax.all_to_all(outgoing, DEV, split_axis=0, concat_axis=0, tiled=True)  9.2 us
  transfers between devices with their start and end apart: 5, of which 4 were waited for; matrix products, arithmetic and copies ran while one was open for 8% of the time, Pallas kernels for 0%

commit v1 on v0

v1 whole, which is shorter than its diff:
```python
import jax
import jax.numpy as jnp
from jax import lax
from jax.experimental import pallas as pl
from jax.experimental.pallas import tpu as pltpu
from jax.sharding import Mesh
from jax.sharding import PartitionSpec as P

DEV = ("dev_0", "dev_1", "dev_2", "dev_3")
LOG2E = 1.4426950408889634
SPREAD = 35.0
TINY = 1e-12
K, B, NB, CAP, N = 256, 512, 32, 16, 128
G = 128
ROW = B + K + G


def split3(row):
    hi = row.astype(jnp.bfloat16).astype(jnp.float32)
    mid = (row - hi).astype(jnp.bfloat16).astype(jnp.float32)
    low = row - hi - mid
    index = lax.broadcasted_iota(jnp.int32, (8, row.shape[1]), 0)
    rows = jnp.where(index == 0, hi, jnp.where(index == 1, mid, jnp.where(index == 2, low, 0.0)))
    return rows.astype(jnp.bfloat16)


def column_sums(weights, e_ref, at):
    parts = lax.dot_general(
        weights, e_ref[:, pl.ds(at, B)], (((1,), (0,)), ((), ())), preferred_element_type=jnp.float32
    )
    return parts[0:1] + parts[1:2] + parts[2:3]


def add_totals(acc_ref, e_ref, at, inverse):
    spread = [jnp.broadcast_to(inverse[:, g * G : (g + 1) * G], (16, G)) for g in range(B // G)]
    for c in range(K // 16):
        rows = slice(16 * c, 16 * c + 16)
        part = acc_ref[rows, :]
        for g in range(B // G):
            part = part + e_ref[rows, pl.ds(at + g * G, G)].astype(jnp.float32) * spread[g]
        acc_ref[rows, :] = part


def rows_of(acc):
    out = lax.dot_general(
        jnp.ones((8, G), jnp.float32),
        acc,
        (((1,), (1,)), ((), ())),
        preferred_element_type=jnp.float32,
        precision=lax.Precision.HIGHEST,
    )
    return out[0:1]


def live_lanes(live_ref, b):
    return lax.broadcasted_iota(jnp.int32, (1, B), 1) < live_ref[b]


def careful(off, live_ref, e_hbm, buf, sem, ld_ref, acc_ref):
    eye = lax.broadcasted_iota(jnp.int32, (K, K), 0) == lax.broadcasted_iota(jnp.int32, (K, K), 1)
    column = jnp.sum(jnp.where(eye, jnp.broadcast_to(off, (K, K)), 0.0), axis=1, keepdims=True)
    acc_ref[...] = jnp.zeros_like(acc_ref)

    @pl.loop(0, NB)
    def _(b):
        @pl.when(live_ref[b] > 0)
        def _():
            copy = pltpu.make_async_copy(e_hbm.at[:, pl.ds(pl.multiple_of(b * B, B), B)], buf, sem)
            copy.start()
            copy.wait()
            for g in range(B // G):
                lanes = slice(g * G, (g + 1) * G)
                shifted = column - buf[:, lanes].astype(jnp.float32)
                top = jnp.max(shifted, axis=0, keepdims=True)
                log_denom = top + jnp.log(jnp.sum(jnp.exp(shifted - top), axis=0, keepdims=True))
                live = lax.broadcasted_iota(jnp.int32, (1, G), 1) + g * G < live_ref[b]
                if ld_ref is not None:
                    ld_ref[b, :, lanes] = jnp.where(live, log_denom, 0.0)
                acc_ref[...] += jnp.where(live, jnp.exp(shifted - log_denom), 0.0)


def first_kernel(live_ref, off_ref, e_hbm, e0_ref, e1_ref, emin_ref, send_ref, acc_ref, tot_ref, buf, sems, sem):
    halves = (e0_ref, e1_ref)

    def copy_of(b, half):
        return pltpu.make_async_copy(
            e_hbm.at[:, pl.ds(pl.multiple_of(b * B, B), B)],
            halves[half].at[:, pl.ds(pl.multiple_of(b // 2 * B, B), B)],
            sems.at[b],
        )

    for b in range(NB):
        copy_of(b, b % 2).start()
    off = off_ref[...]
    scaled = jnp.exp(off - jnp.max(off))
    weights = split3(scaled)
    acc_ref[...] = jnp.zeros_like(acc_ref)

    def exponentials(i, half):
        b = 2 * i + half
        copy_of(b, half).wait()
        ref = halves[half]
        at = pl.multiple_of(i * B, B)
        for g in range(B // G):
            lanes = pl.ds(at + g * G, G)
            low = ref[0:16, lanes]
            for c in range(1, K // 16):
                low = jnp.minimum(low, ref[16 * c : 16 * c + 16, lanes])
            row = jnp.min(low.astype(jnp.float32), axis=0, keepdims=True)
            emin_ref[b, :, g * G : (g + 1) * G] = row
            wide = jnp.broadcast_to(row, (16, G))
            for c in range(K // 16):
                rows = slice(16 * c, 16 * c + 16)
                value = jnp.exp2((wide - ref[rows, lanes].astype(jnp.float32)) * LOG2E)
                ref[rows, lanes] = value.astype(jnp.bfloat16)

    def totals(i, half):
        b = 2 * i + half
        at = pl.multiple_of(i * B, B)
        sums = column_sums(weights, halves[half], at)
        inverse = jnp.where(live_lanes(live_ref, b), 1.0 / sums, 0.0)
        add_totals(acc_ref, halves[half], at, inverse)

    exponentials(0, 0)

    @pl.loop(0, NB // 2 - 1)
    def _(i):
        exponentials(i, 1)
        totals(i, 0)
        exponentials(i + 1, 0)
        totals(i, 1)

    exponentials(NB // 2 - 1, 1)
    totals(NB // 2 - 1, 0)
    totals(NB // 2 - 1, 1)
    tot_ref[...] = rows_of(acc_ref[...]) * scaled

    @pl.when(jnp.min(tot_ref[...]) < TINY)
    def _():
        careful(off, live_ref, e_hbm, buf, sem, None, acc_ref)
        tot_ref[...] = rows_of(acc_ref[...])

    send_ref[...] = jnp.broadcast_to(tot_ref[...][None], (N, 1, K))


def second_kernel(
    live_ref, owner_ref, slot_ref, lc_ref, off1_ref, got_ref, e_hbm, e0_ref, e1_ref, emin_ref,
    send_ref, home_ref, off_ref, acc_ref, ld_ref, tot_ref, buf, sem,
):
    halves = (e0_ref, e1_ref)
    updated = off1_ref[...] - jnp.log(jnp.sum(got_ref[:, 0, :], axis=0, keepdims=True))
    off = lc_ref[...] + (updated - updated[:, 0:1])
    off_ref[...] = off
    top = jnp.max(off)
    spread = top - jnp.min(off)
    scaled = jnp.exp(off - top)
    weights = split3(scaled)
    acc_ref[...] = jnp.zeros_like(acc_ref)

    def denominators(i, half):
        b = 2 * i + half
        at = pl.multiple_of(i * B, B)
        sums = column_sums(weights, halves[half], at)
        live = live_lanes(live_ref, b)
        ld_ref[b] = jnp.where(live, jnp.log(sums) + top - emin_ref[b], 0.0)
        return jnp.where(live, 1.0 / sums, 0.0)

    def totals(i, half, inverse):
        add_totals(acc_ref, halves[half], pl.multiple_of(i * B, B), inverse)

    def body(i, inverse):
        other = denominators(i, 1)
        totals(i, 0, inverse)
        inverse = denominators(i + 1, 0)
        totals(i, 1, other)
        return inverse

    inverse = lax.fori_loop(0, NB // 2 - 1, body, denominators(0, 0))
    other = denominators(NB // 2 - 1, 1)
    totals(NB // 2 - 1, 0, inverse)
    totals(NB // 2 - 1, 1, other)
    tot_ref[...] = rows_of(acc_ref[...]) * scaled

    @pl.when((jnp.min(tot_ref[...]) < TINY) | (spread > SPREAD))
    def _():
        careful(off, live_ref, e_hbm, buf, sem, ld_ref, acc_ref)
        tot_ref[...] = rows_of(acc_ref[...])

    send_ref[:, :, 0:B] = jnp.zeros((N, 1, B), jnp.float32)
    send_ref[:, :, B : B + K] = jnp.broadcast_to(tot_ref[...][None], (N, 1, K))
    send_ref[:, :, B + K :] = jnp.full((N, 1, G), -1.0, jnp.float32)
    home_ref[...] = jnp.zeros_like(home_ref)
    me = lax.axis_index(DEV)

    @pl.loop(0, NB)
    def _(b):
        owner = owner_ref[b]
        slot = slot_ref[b]

        @pl.when((live_ref[b] > 0) & (owner == me))
        def _():
            home_ref[slot] = ld_ref[b]

        @pl.when((live_ref[b] > 0) & (owner != me))
        def _():
            send_ref[owner, :, 0:B] = ld_ref[b]
            send_ref[owner, :, B + K :] = jnp.full((1, G), slot.astype(jnp.float32))


def third_kernel(got_ref, home_ref, off_ref, free_ref, out_ref):
    total = jnp.sum(got_ref[:, 0, B : B + K], axis=0, keepdims=True)
    updated = off_ref[...] - jnp.log(total)
    free_ref[...] = updated - updated[:, 0:1]
    lane = lax.broadcasted_iota(jnp.int32, (N, G), 1).astype(jnp.float32)
    chosen = jnp.where(got_ref[:, 0, B + K :] == lane, 1.0, 0.0)
    rows = lax.dot_general(
        chosen,
        got_ref[:, 0, 0:B],
        (((0,), (0,)), ((), ())),
        preferred_element_type=jnp.float32,
        precision=lax.Precision.HIGHEST,
    )
    out_ref[...] = home_ref[:, 0, :] + rows[0:CAP]


VMEM = pl.BlockSpec(memory_space=pltpu.VMEM)
SMEM = pl.BlockSpec(memory_space=pltpu.SMEM)
HBM = pl.BlockSpec(memory_space=pltpu.HBM)


def f32(*shape):
    return jax.ShapeDtypeStruct(shape, jnp.float32)


def body(energies, block_live_samples, block_owner, block_slot, state_counts, start_free):
    params = pltpu.CompilerParams(vmem_limit_bytes=16 * 1024 * 1024)
    energies = pltpu.with_memory_space_constraint(energies, pltpu.HBM)
    log_counts = jnp.log(state_counts.astype(jnp.float32))
    offsets = (log_counts + start_free)[None]
    half = jax.ShapeDtypeStruct((K, NB // 2 * B), jnp.bfloat16)
    e0, e1, emin, total = pl.pallas_call(
        first_kernel,
        out_shape=(half, half, f32(NB, 1, B), f32(N, 1, K)),
        in_specs=[SMEM, VMEM, HBM],
        out_specs=(VMEM, VMEM, VMEM, VMEM),
        scratch_shapes=[
            pltpu.VMEM((K, G), jnp.float32),
            pltpu.VMEM((1, K), jnp.float32),
            pltpu.VMEM((K, B), jnp.bfloat16),
            pltpu.SemaphoreType.DMA((NB,)),
            pltpu.SemaphoreType.DMA,
        ],
        compiler_params=params,
        name="first",
    )(block_live_samples, offsets, energies)
    parts = lax.all_to_all(total, DEV, 0, 0, tiled=True)
    send, home, offsets = pl.pallas_call(
        second_kernel,
        out_shape=(f32(N, 1, ROW), f32(CAP, 1, B), f32(1, K)),
        in_specs=[SMEM, SMEM, SMEM, VMEM, VMEM, VMEM, HBM, VMEM, VMEM, VMEM],
        out_specs=(VMEM, VMEM, VMEM),
        scratch_shapes=[
            pltpu.VMEM((K, G), jnp.float32),
            pltpu.VMEM((NB, 1, B), jnp.float32),
            pltpu.VMEM((1, K), jnp.float32),
            pltpu.VMEM((K, B), jnp.bfloat16),
            pltpu.SemaphoreType.DMA,
        ],
        compiler_params=params,
        name="second",
    )(block_live_samples, block_owner, block_slot, log_counts[None], offsets, parts, energies, e0, e1, emin)
    got = lax.all_to_all(send, DEV, 0, 0, tiled=True)
    free, placed = pl.pallas_call(
        third_kernel,
        out_shape=(f32(1, K), f32(CAP, B)),
        in_specs=[VMEM, VMEM, VMEM],
        out_specs=(VMEM, VMEM),
        compiler_params=params,
        name="third",
    )(got, home, offsets)
    return free[0], placed


def solution(mesh):
    split = Mesh(mesh.devices.reshape(4, 4, 4, 2), DEV)
    return jax.shard_map(
        body,
        mesh=split,
        in_specs=(P(None, DEV), P(DEV), P(DEV), P(DEV), P(), P()),
        out_specs=(P(), P(DEV, None)),
        check_vma=False,
    )
```

time: 114 us -> 60.3 us (0.53)
  other arithmetic: 38.8 us -> 0.7 us
  blocking collectives: 5.84 us -> 39 us
  waiting for transfers between devices: 30.3 us -> 0 us
  starting transfers between devices: 29.7 us -> 0 us
  Pallas kernels: 0 us -> 19.3 us
  local copies, waits for them, and re-layouts: 7.96 us -> 0.67 us
    all_to_all x1 -> x2, blocking collectives: 5.84 us -> 39 us  [the longest x1 21.6 us: body(): parts = lax.all_to_all(total, DEV, 0, 0, tiled=True)]
    all_to_all x5 -> x0, waiting for transfers between devices: 30.3 us -> none  [the longest x3 11.6 us: copy_for_each(): lax.all_to_all(jnp.broadcast_to(value[None], (size, *value.shape)), axis,...]
    all_to_all x5 -> x0, starting transfers between devices: 29.7 us -> none  [the longest x3 14.1 us: copy_for_each(): lax.all_to_all(jnp.broadcast_to(value[None], (size, *value.shape)), axis,...]
    reduce_sum x11 -> x0, other arithmetic: 20.9 us -> none  [the longest x2 10.4 us: block_pass(): jnp.sum(jnp.exp(shifted - largest[None]), axis=0)]
    pallas_call x0 -> x3, Pallas kernels: none -> 19.3 us  [the longest x1 11.8 us: body(): pl.pallas_call(first_kernel, out_shape=(half, half, f32(NB, 1, B), f32(N,...]
    reduce_max x2 -> x0, other arithmetic: 11.5 us -> none  [block_pass(): largest = jnp.max(shifted, axis=0)]
    gather x4 -> x0, local copies, waits for them, and re-layouts: 3.13 us -> none  [the longest x1 1.23 us: body(): out_slot = jnp.where(present, block_slot[source], -1)[:, None]]
    all_to_all x1 -> x0, other arithmetic: 2.35 us -> none  [body(): lax.all_to_all(out_slot, DEV, split_axis=0, concat_axis=0, tiled=True)]
  transfers between devices with their start and end apart: 5 -> 0, of which waited for: 4 -> 0; matrix products, arithmetic and copies ran while one was open for 8% -> 0% of each run, Pallas kernels for 0% -> 0%
where the time goes in v1:
time: 60.3 us
  blocking collectives  39 us (65%)
  Pallas kernels  19.3 us (32%)
  other arithmetic  0.7 us (1%)
  local copies, waits for them, and re-layouts  0.67 us (1%)
  between operations  0.65 us (1%)
    all_to_all x1, blocking collectives, body(): parts = lax.all_to_all(total, DEV, 0, 0, tiled=True)  21.6 us
    all_to_all x1, blocking collectives, body(): got = lax.all_to_all(send, DEV, 0, 0, tiled=True)  17.3 us
    pallas_call x1, Pallas kernels, body(): pl.pallas_call(first_kernel, out_shape=(half, half, f32(NB, 1, B), f32(N,...  11.8 us
    pallas_call x1, Pallas kernels, body(): pl.pallas_call(second_kernel, out_shape=(f32(N, 1, ROW), f32(CAP, 1, B),...  6.47 us

profile of v1, /device:TPU:1, one launch (start us, length us, event | category | flops | bytes accessed | tf_op | source)
XLA Modules:
  0.0 60.3 jit_solution(4277528672973833958)
XLA Ops:
  0.6 0.7 %fusion = (f32[256]{0:T(256)S(1)}, f32[256]{0:T(256)S(1)}) fusion(f32[256]{0:T(256)} %param.11, s32[256]{0:T(256)} %param.10), kind=kLoop, calls=%fused_computation.1 | loop fusion | flops 512 | bytes 4096 | tf_op jit(solution)/shard_map/add | solution.py:239
  1.3 0.0 copy-start
  1.3 0.7 %copy-done = s32[32]{0:T(128)S(1)} copy-done((s32[32]{0:T(128)S(1)}, s32[32]{0:T(128)}, u32[]{:S(2)}) %copy-start) | copy-done | bytes 152
  2.0 0.0 copy-start.1
  2.0 0.0 copy-start.2
  2.0 11.8 %first.1 = (bf16[256,8192]{1,0:T(8,128)(2,1)S(1)}, bf16[256,8192]{1,0:T(8,128)(2,1)S(1)}, f32[32,1,512]{2,1,0:T(1,128)S(1)}, f32[128,1,256]{2,1,0:T(1,128)S(1)}) custom-call(s32[32]{0:T(128)S(1)} %copy-done, f32[1,256]{1,0:T(1,128)S(1)} %bitcast.3, bf16[256,16384]{1,0:T(8,128)(2,1)} %e_hbm.3), custom_call_target="tpu_custom_call" | custom-call | tf_op jit(solution)/shard_map/first/pallas_call | solution.py:241
  13.8 21.6 %all_to_all.10.got_ref = f32[128,1,256]{2,1,0:T(1,128)S(1)} all-to-all(f32[128,1,256]{2,1,0:T(1,128)S(1)} %get-tuple-element.11), channel_id=1, replica_groups=mesh['dev_0'=4,'dev_1'=4,'dev_2'=4,'dev_3'=2] {'dev_0','dev_1','dev_2','..., dimensions={0} | all-to-all | bytes 262144 | tf_op jit(solution)/shard_map/all_to_all | solution.py:256
  35.4 0.0 copy-done.1
  35.4 0.0 copy-done.2
  35.4 6.5 %second.1 = (f32[128,1,896]{2,1,0:T(1,128)S(1)}, f32[16,1,512]{2,1,0:T(1,128)S(1)}, f32[1,256]{1,0:T(1,128)S(1)}) custom-call(s32[32]{0:T(128)S(1)} %copy-done, s32[32]{0:T(128)S(1)} %copy-done.1, s32[32]{0:T(128)S(1)} %copy-done.2, f32[1,256]{1,0:T(1,128)S(1)} %bitcast.5, f32[1,256]{1,0:T(1,128)S(1)} %bitcast.4, f32[128,1,256]{2,1,0:T(1,128)S(1)} %all_to_all.10.got_ref, ...), custom_call_target="tpu_custom_call" | custom-call | tf_op jit(solution)/shard_map/second/pallas_call | solution.py:257
  41.9 17.3 %all_to_all.11.got_ref = f32[128,1,896]{2,1,0:T(1,128)S(1)} all-to-all(f32[128,1,896]{2,1,0:T(1,128)S(1)} %get-tuple-element.15), channel_id=1, replica_groups=mesh['dev_0'=4,'dev_1'=4,'dev_2'=4,'dev_3'=2] {'dev_0','dev_1','dev_2','..., dimensions={0} | all-to-all | bytes 917504 | tf_op jit(solution)/shard_map/all_to_all | solution.py:272
  59.2 1.0 %third.1 = (f32[1,256]{1,0:T(1,128)}, f32[16,512]{1,0:T(8,128)}) custom-call(f32[128,1,896]{2,1,0:T(1,128)S(1)} %all_to_all.11.got_ref, f32[16,1,512]{2,1,0:T(1,128)S(1)} %get-tuple-element.16.home_ref, f32[1,256]{1,0:T(1,128)S(1)} %get-tuple-element.17.off_ref), custom_call_target="tpu_custom_call" | custom-call | tf_op jit(solution)/shard_map/third/pallas_call | solution.py:273
Async XLA Ops:
  1.3 0.7 %copy-start = (s32[32]{0:T(128)S(1)}, s32[32]{0:T(128)}, u32[]{:S(2)}) copy-start(s32[32]{0:T(128)} %live_ref.3) | copy-start | bytes 388
  2.0 33.5 %copy-start.1 = (s32[32]{0:T(128)S(1)}, s32[32]{0:T(128)}, u32[]{:S(2)}) copy-start(s32[32]{0:T(128)} %owner_ref.1) | copy-start | bytes 388
  2.0 33.5 %copy-start.2 = (s32[32]{0:T(128)S(1)}, s32[32]{0:T(128)}, u32[]{:S(2)}) copy-start(s32[32]{0:T(128)} %slot_ref.1) | copy-start | bytes 388

commit v2 on v1

--- a/solution.py
+++ b/solution.py
@@ -10,34 +10,39 @@
 LOG2E = 1.4426950408889634
 SPREAD = 35.0
 TINY = 1e-12
+AHEAD = 8
+LARGE = 5e21
 K, B, NB, CAP, N = 256, 512, 32, 16, 128
 G = 128
 ROW = B + K + G
 
 
-def split3(row):
-    hi = row.astype(jnp.bfloat16).astype(jnp.float32)
-    mid = (row - hi).astype(jnp.bfloat16).astype(jnp.float32)
-    low = row - hi - mid
-    index = lax.broadcasted_iota(jnp.int32, (8, row.shape[1]), 0)
-    rows = jnp.where(index == 0, hi, jnp.where(index == 1, mid, jnp.where(index == 2, low, 0.0)))
-    return rows.astype(jnp.bfloat16)
-
-
-def column_sums(weights, e_ref, at):
-    parts = lax.dot_general(
-        weights, e_ref[:, pl.ds(at, B)], (((1,), (0,)), ((), ())), preferred_element_type=jnp.float32
-    )
-    return parts[0:1] + parts[1:2] + parts[2:3]
+def down_lanes(row):
+    return jnp.transpose(jnp.broadcast_to(row, (G, K)))
+
+
+def as_row(sums):
+    return jnp.concatenate([jnp.sum(part, axis=0, keepdims=True) for part in sums], axis=1)
+
+
+def column_sums(w_ref, e_ref, at):
+    sums = [None] * (B // G)
+    for c in range(K // 8):
+        rows = slice(8 * c, 8 * c + 8)
+        weight = w_ref[rows, :]
+        for g in range(B // G):
+            term = e_ref[at, rows, g * G : (g + 1) * G] * weight
+            sums[g] = term if c == 0 else sums[g] + term
+    return as_row(sums)
 
 
 def add_totals(acc_ref, e_ref, at, inverse):
-    spread = [jnp.broadcast_to(inverse[:, g * G : (g + 1) * G], (16, G)) for g in range(B // G)]
-    for c in range(K // 16):
-        rows = slice(16 * c, 16 * c + 16)
+    spread = [jnp.broadcast_to(inverse[:, g * G : (g + 1) * G], (8, G)) for g in range(B // G)]
+    for c in range(K // 8):
+        rows = slice(8 * c, 8 * c + 8)
         part = acc_ref[rows, :]
         for g in range(B // G):
-            part = part + e_ref[rows, pl.ds(at + g * G, G)].astype(jnp.float32) * spread[g]
+            part = part + e_ref[at, rows, g * G : (g + 1) * G] * spread[g]
         acc_ref[rows, :] = part
 
 
@@ -79,61 +84,89 @@
                 acc_ref[...] += jnp.where(live, jnp.exp(shifted - log_denom), 0.0)
 
 
-def first_kernel(live_ref, off_ref, e_hbm, e0_ref, e1_ref, emin_ref, send_ref, acc_ref, tot_ref, buf, sems, sem):
+def first_kernel(
+    live_hbm, counts_hbm, free_hbm, e_hbm,
+    e0_ref, e1_ref, emin_ref, send_ref, lc_ref, off_ref,
+    acc_ref, w_ref, tot_ref, bad_ref, inv_ref, raw, buf, counts, live_ref, sems, small, sem,
+):
     halves = (e0_ref, e1_ref)
 
-    def copy_of(b, half):
-        return pltpu.make_async_copy(
-            e_hbm.at[:, pl.ds(pl.multiple_of(b * B, B), B)],
-            halves[half].at[:, pl.ds(pl.multiple_of(b // 2 * B, B), B)],
-            sems.at[b],
-        )
-
-    for b in range(NB):
-        copy_of(b, b % 2).start()
-    off = off_ref[...]
+    def copy_of(b):
+        return pltpu.make_async_copy(e_hbm.at[:, pl.ds(pl.multiple_of(b * B, B), B)], raw.at[b], sems.at[b])
+
+    staged = [
+        pltpu.make_async_copy(counts_hbm, counts, small.at[0]),
+        pltpu.make_async_copy(free_hbm, off_ref, small.at[1]),
+        pltpu.make_async_copy(live_hbm, live_ref, small.at[2]),
+    ]
+    for copy in staged:
+        copy.start()
+    for b in range(AHEAD):
+        copy_of(b).start()
+    for copy in staged:
+        copy.wait()
+    lc_ref[...] = jnp.log(counts[...].astype(jnp.float32))
+    off = lc_ref[...] + off_ref[...]
+    off_ref[...] = off
     scaled = jnp.exp(off - jnp.max(off))
-    weights = split3(scaled)
-    acc_ref[...] = jnp.zeros_like(acc_ref)
-
-    def exponentials(i, half):
+    w_ref[...] = down_lanes(scaled)
+
+    def exponentials(i, half, first):
         b = 2 * i + half
-        copy_of(b, half).wait()
-        ref = halves[half]
-        at = pl.multiple_of(i * B, B)
-        for g in range(B // G):
-            lanes = pl.ds(at + g * G, G)
-            low = ref[0:16, lanes]
-            for c in range(1, K // 16):
-                low = jnp.minimum(low, ref[16 * c : 16 * c + 16, lanes])
-            row = jnp.min(low.astype(jnp.float32), axis=0, keepdims=True)
-            emin_ref[b, :, g * G : (g + 1) * G] = row
-            wide = jnp.broadcast_to(row, (16, G))
-            for c in range(K // 16):
-                rows = slice(16 * c, 16 * c + 16)
-                value = jnp.exp2((wide - ref[rows, lanes].astype(jnp.float32)) * LOG2E)
-                ref[rows, lanes] = value.astype(jnp.bfloat16)
+        if first:
+            copy_of(b).wait()
+
+            @pl.when(b + AHEAD < NB)
+            def _():
+                copy_of(b + AHEAD).start()
+
+        else:
+            low = jnp.min(raw[b].astype(jnp.float32), axis=0, keepdims=True)
+            emin_ref[b] = low
+            shift = jnp.broadcast_to(low, (8, B))
+        sums = [None] * (B // G)
+        for c in range(K // 8):
+            rows = slice(8 * c, 8 * c + 8)
+            weight = w_ref[rows, :]
+            for g in range(B // G):
+                energy = raw[b, rows, g * G : (g + 1) * G].astype(jnp.float32)
+                if first:
+                    value = jnp.exp2(energy * -LOG2E)
+                else:
+                    value = jnp.exp2((shift[:, g * G : (g + 1) * G] - energy) * LOG2E)
+                halves[half][i, rows, g * G : (g + 1) * G] = value
+                term = value * weight
+                sums[g] = term if c == 0 else sums[g] + term
+        total = as_row(sums)
+        bad_ref[...] = jnp.where(total <= LARGE, bad_ref[...], 1.0)
+        inv_ref[half : half + 1] = jnp.where(live_lanes(live_ref, b), 1.0 / total, 0.0)
 
     def totals(i, half):
-        b = 2 * i + half
-        at = pl.multiple_of(i * B, B)
-        sums = column_sums(weights, halves[half], at)
-        inverse = jnp.where(live_lanes(live_ref, b), 1.0 / sums, 0.0)
-        add_totals(acc_ref, halves[half], at, inverse)
-
-    exponentials(0, 0)
-
-    @pl.loop(0, NB // 2 - 1)
-    def _(i):
-        exponentials(i, 1)
-        totals(i, 0)
-        exponentials(i + 1, 0)
-        totals(i, 1)
-
-    exponentials(NB // 2 - 1, 1)
-    totals(NB // 2 - 1, 0)
-    totals(NB // 2 - 1, 1)
-    tot_ref[...] = rows_of(acc_ref[...]) * scaled
+        add_totals(acc_ref, halves[half], i, inv_ref[half : half + 1])
+
+    def sweep(first):
+        acc_ref[...] = jnp.zeros_like(acc_ref)
+        exponentials(0, 0, first)
+
+        @pl.loop(0, NB // 2 - 1)
+        def _(i):
+            exponentials(i, 1, first)
+            totals(i, 0)
+            exponentials(i + 1, 0, first)
+            totals(i, 1)
+
+        exponentials(NB // 2 - 1, 1, first)
+        totals(NB // 2 - 1, 0)
+        totals(NB // 2 - 1, 1)
+        tot_ref[...] = rows_of(acc_ref[...]) * scaled
+
+    bad_ref[...] = jnp.zeros_like(bad_ref)
+    emin_ref[...] = jnp.zeros_like(emin_ref)
+    sweep(True)
+
+    @pl.when(jnp.max(bad_ref[...]) > 0.0)
+    def _():
+        sweep(False)
 
     @pl.when(jnp.min(tot_ref[...]) < TINY)
     def _():
@@ -145,7 +178,7 @@
 
 def second_kernel(
     live_ref, owner_ref, slot_ref, lc_ref, off1_ref, got_ref, e_hbm, e0_ref, e1_ref, emin_ref,
-    send_ref, home_ref, off_ref, acc_ref, ld_ref, tot_ref, buf, sem,
+    send_ref, home_ref, off_ref, acc_ref, w_ref, ld_ref, tot_ref, buf, sem,
 ):
     halves = (e0_ref, e1_ref)
     updated = off1_ref[...] - jnp.log(jnp.sum(got_ref[:, 0, :], axis=0, keepdims=True))
@@ -154,19 +187,18 @@
     top = jnp.max(off)
     spread = top - jnp.min(off)
     scaled = jnp.exp(off - top)
-    weights = split3(scaled)
+    w_ref[...] = down_lanes(scaled)
     acc_ref[...] = jnp.zeros_like(acc_ref)
 
     def denominators(i, half):
         b = 2 * i + half
-        at = pl.multiple_of(i * B, B)
-        sums = column_sums(weights, halves[half], at)
+        sums = column_sums(w_ref, halves[half], i)
         live = live_lanes(live_ref, b)
         ld_ref[b] = jnp.where(live, jnp.log(sums) + top - emin_ref[b], 0.0)
         return jnp.where(live, 1.0 / sums, 0.0)
 
     def totals(i, half, inverse):
-        add_totals(acc_ref, halves[half], pl.multiple_of(i * B, B), inverse)
+        add_totals(acc_ref, halves[half], i, inverse)
 
     def body(i, inverse):
         other = denominators(i, 1)
@@ -234,25 +266,33 @@
 
 def body(energies, block_live_samples, block_owner, block_slot, state_counts, start_free):
     params = pltpu.CompilerParams(vmem_limit_bytes=16 * 1024 * 1024)
-    energies = pltpu.with_memory_space_constraint(energies, pltpu.HBM)
-    log_counts = jnp.log(state_counts.astype(jnp.float32))
-    offsets = (log_counts + start_free)[None]
-    half = jax.ShapeDtypeStruct((K, NB // 2 * B), jnp.bfloat16)
-    e0, e1, emin, total = pl.pallas_call(
+    energies, live, counts, start = (
+        pltpu.with_memory_space_constraint(value, pltpu.HBM)
+        for value in (energies, block_live_samples, state_counts[None], start_free[None])
+    )
+    half = f32(NB // 2, K, B)
+    e0, e1, emin, total, log_counts, offsets = pl.pallas_call(
         first_kernel,
-        out_shape=(half, half, f32(NB, 1, B), f32(N, 1, K)),
-        in_specs=[SMEM, VMEM, HBM],
-        out_specs=(VMEM, VMEM, VMEM, VMEM),
+        out_shape=(half, half, f32(NB, 1, B), f32(N, 1, K), f32(1, K), f32(1, K)),
+        in_specs=[HBM, HBM, HBM, HBM],
+        out_specs=(VMEM,) * 6,
         scratch_shapes=[
             pltpu.VMEM((K, G), jnp.float32),
+            pltpu.VMEM((K, G), jnp.float32),
             pltpu.VMEM((1, K), jnp.float32),
+            pltpu.VMEM((1, B), jnp.float32),
+            pltpu.VMEM((2, B), jnp.float32),
+            pltpu.VMEM((NB, K, B), jnp.bfloat16),
             pltpu.VMEM((K, B), jnp.bfloat16),
+            pltpu.VMEM((1, K), jnp.int32),
+            pltpu.SMEM((NB,), jnp.int32),
             pltpu.SemaphoreType.DMA((NB,)),
+            pltpu.SemaphoreType.DMA((3,)),
             pltpu.SemaphoreType.DMA,
         ],
         compiler_params=params,
         name="first",
-    )(block_live_samples, offsets, energies)
+    )(live, counts, start, energies)
     parts = lax.all_to_all(total, DEV, 0, 0, tiled=True)
     send, home, offsets = pl.pallas_call(
         second_kernel,
@@ -261,6 +301,7 @@
         out_specs=(VMEM, VMEM, VMEM),
         scratch_shapes=[
             pltpu.VMEM((K, G), jnp.float32),
+            pltpu.VMEM((K, G), jnp.float32),
             pltpu.VMEM((NB, 1, B), jnp.float32),
             pltpu.VMEM((1, K), jnp.float32),
             pltpu.VMEM((K, B), jnp.bfloat16),
@@ -268,7 +309,7 @@
         ],
         compiler_params=params,
         name="second",
-    )(block_live_samples, block_owner, block_slot, log_counts[None], offsets, parts, energies, e0, e1, emin)
+    )(block_live_samples, block_owner, block_slot, log_counts, offsets, parts, energies, e0, e1, emin)
     got = lax.all_to_all(send, DEV, 0, 0, tiled=True)
     free, placed = pl.pallas_call(
         third_kernel,

time: 60.3 us -> 59.7 us (0.990)
  other arithmetic: 0.7 us -> 0 us
  local copies, waits for them, and re-layouts: 0.67 us -> 0.01 us
    pallas_call x1, Pallas kernels: 6.47 us -> 5.14 us  [body(): pl.pallas_call(second_kernel, out_shape=(f32(N, 1, ROW), f32(CAP, 1, B),...]
    pallas_call x1, Pallas kernels: 11.8 us -> 13 us  [body(): pl.pallas_call(first_kernel, out_shape=(half, half, f32(NB, 1, B), f32(N,...]
    add x1 -> x0, other arithmetic: 0.7 us -> none  [body(): offsets = (log_counts + start_free)[None]]
    unnamed x6, local copies, waits for them, and re-layouts: 0.67 us -> 0.01 us
where the time goes in v2:
time: 59.7 us; the launch traced here: 59.3 us
  blocking collectives  39.5 us (66%)
  Pallas kernels  19.1 us (32%)
  between operations  0.68 us (1%)
    all_to_all x1, blocking collectives, body(): parts = lax.all_to_all(total, DEV, 0, 0, tiled=True)  21.7 us
    all_to_all x1, blocking collectives, body(): got = lax.all_to_all(send, DEV, 0, 0, tiled=True)  17.9 us
    pallas_call x1, Pallas kernels, body(): pl.pallas_call(first_kernel, out_shape=(half, half, f32(NB, 1, B), f32(N,...  13 us
    pallas_call x1, Pallas kernels, body(): pl.pallas_call(second_kernel, out_shape=(f32(N, 1, ROW), f32(CAP, 1, B),...  5.14 us

profile of v2, /device:TPU:1, one launch (start us, length us, event | category | flops | bytes accessed | tf_op | source)
XLA Modules:
  0.0 59.3 jit_solution(4079872986137283502)
XLA Ops:
  0.6 0.0 copy-start
  0.6 0.0 copy-start.2
  0.7 0.0 copy-start.1
  0.7 13.0 %first.1 = (f32[16,256,512]{2,1,0:T(8,128)S(1)}, f32[16,256,512]{2,1,0:T(8,128)S(1)}, f32[32,1,512]{2,1,0:T(1,128)S(1)}, f32[128,1,256]{2,1,0:T(1,128)S(1)}, f32[1,256]{1,0:T(1,128)S(1)}, /*index=5*/f32[1,256]{1,0:T(1,128)S(1)}) custom-call(s32[32]{0:T(128)} %live_ref.1, s32[1,256]{1,0:T(1,128)} %bitcast.3, f32[1,256]{1,0:T(1,128)} %bitcast.4, ...), custom_call_target="tpu_custom_call" | custom-call | tf_op jit(solution)/shard_map/first/pallas_call | solution.py:274
  13.6 21.7 %all_to_all.10.got_ref = f32[128,1,256]{2,1,0:T(1,128)S(1)} all-to-all(f32[128,1,256]{2,1,0:T(1,128)S(1)} %get-tuple-element.15), channel_id=1, replica_groups=mesh['dev_0'=4,'dev_1'=4,'dev_2'=4,'dev_3'=2] {'dev_0','dev_1','dev_2','..., dimensions={0} | all-to-all | bytes 262144 | tf_op jit(solution)/shard_map/all_to_all | solution.py:296
  35.3 0.0 copy-done
  35.3 0.0 copy-done.2
  35.3 0.0 copy-done.1
  35.3 5.1 %second.1 = (f32[128,1,896]{2,1,0:T(1,128)S(1)}, f32[16,1,512]{2,1,0:T(1,128)S(1)}, f32[1,256]{1,0:T(1,128)S(1)}) custom-call(s32[32]{0:T(128)S(1)} %copy-done, s32[32]{0:T(128)S(1)} %copy-done.1, s32[32]{0:T(128)S(1)} %copy-done.2, f32[1,256]{1,0:T(1,128)S(1)} %get-tuple-element.13.lc_ref, f32[1,256]{1,0:T(1,128)S(1)} %get-tuple-element.14.off1_ref, ...), custom_call_target="tpu_custom_call" | custom-call | tf_op jit(solution)/shard_map/second/pallas_call | solution.py:297
  40.5 17.9 %all_to_all.11.got_ref = f32[128,1,896]{2,1,0:T(1,128)S(1)} all-to-all(f32[128,1,896]{2,1,0:T(1,128)S(1)} %get-tuple-element.19), channel_id=1, replica_groups=mesh['dev_0'=4,'dev_1'=4,'dev_2'=4,'dev_3'=2] {'dev_0','dev_1','dev_2','..., dimensions={0} | all-to-all | bytes 917504 | tf_op jit(solution)/shard_map/all_to_all | solution.py:313
  58.3 1.0 %third.1 = (f32[1,256]{1,0:T(1,128)}, f32[16,512]{1,0:T(8,128)}) custom-call(f32[128,1,896]{2,1,0:T(1,128)S(1)} %all_to_all.11.got_ref, f32[16,1,512]{2,1,0:T(1,128)S(1)} %get-tuple-element.20.home_ref, f32[1,256]{1,0:T(1,128)S(1)} %get-tuple-element.21.off_ref), custom_call_target="tpu_custom_call" | custom-call | tf_op jit(solution)/shard_map/third/pallas_call | solution.py:314
Async XLA Ops:
  0.6 34.7 %copy-start = (s32[32]{0:T(128)S(1)}, s32[32]{0:T(128)}, u32[]{:S(2)}) copy-start(s32[32]{0:T(128)} %live_ref.1) | copy-start | bytes 388
  0.6 34.7 %copy-start.2 = (s32[32]{0:T(128)S(1)}, s32[32]{0:T(128)}, u32[]{:S(2)}) copy-start(s32[32]{0:T(128)} %slot_ref.1) | copy-start | bytes 388
  0.7 34.7 %copy-start.1 = (s32[32]{0:T(128)S(1)}, s32[32]{0:T(128)}, u32[]{:S(2)}) copy-start(s32[32]{0:T(128)} %owner_ref.1) | copy-start | bytes 388

commit v3 on v2

--- a/solution.py
+++ b/solution.py
@@ -10,6 +10,7 @@
 LOG2E = 1.4426950408889634
 SPREAD = 35.0
 TINY = 1e-12
+FIRST = 5
 AHEAD = 8
 LARGE = 5e21
 K, B, NB, CAP, N = 256, 512, 32, 16, 128
@@ -47,21 +48,26 @@
 
 
 def rows_of(acc):
-    out = lax.dot_general(
-        jnp.ones((8, G), jnp.float32),
-        acc,
-        (((1,), (1,)), ((), ())),
-        preferred_element_type=jnp.float32,
-        precision=lax.Precision.HIGHEST,
-    )
-    return out[0:1]
+    return jnp.sum(jnp.transpose(acc), axis=0, keepdims=True)
+
+
+def paired(row):
+    even = lax.broadcasted_iota(jnp.int32, (8, G), 0) % 2 == 0
+    return jnp.where(even, jnp.broadcast_to(row[:, :G], (8, G)), jnp.broadcast_to(row[:, G:], (8, G)))
+
+
+def unpaired(got_ref):
+    total = jnp.sum(got_ref[...], axis=0)
+    total = total + pltpu.roll(total, 4, 0)
+    total = total + pltpu.roll(total, 2, 0)
+    return jnp.concatenate([total[0:1], total[1:2]], axis=1)
 
 
 def live_lanes(live_ref, b):
     return lax.broadcasted_iota(jnp.int32, (1, B), 1) < live_ref[b]
 
 
-def careful(off, live_ref, e_hbm, buf, sem, ld_ref, acc_ref):
+def careful(off, live_ref, e_hbm, buf, sem, ld_ref, acc_ref, place=None):
     eye = lax.broadcasted_iota(jnp.int32, (K, K), 0) == lax.broadcasted_iota(jnp.int32, (K, K), 1)
     column = jnp.sum(jnp.where(eye, jnp.broadcast_to(off, (K, K)), 0.0), axis=1, keepdims=True)
     acc_ref[...] = jnp.zeros_like(acc_ref)
@@ -80,8 +86,10 @@
                 log_denom = top + jnp.log(jnp.sum(jnp.exp(shifted - top), axis=0, keepdims=True))
                 live = lax.broadcasted_iota(jnp.int32, (1, G), 1) + g * G < live_ref[b]
                 if ld_ref is not None:
-                    ld_ref[b, :, lanes] = jnp.where(live, log_denom, 0.0)
+                    ld_ref[0, :, lanes] = jnp.where(live, log_denom, 0.0)
                 acc_ref[...] += jnp.where(live, jnp.exp(shifted - log_denom), 0.0)
+            if place is not None:
+                place(b, ld_ref[0])
 
 
 def first_kernel(
@@ -101,7 +109,7 @@
     ]
     for copy in staged:
         copy.start()
-    for b in range(AHEAD):
+    for b in range(FIRST):
         copy_of(b).start()
     for copy in staged:
         copy.wait()
@@ -110,6 +118,8 @@
     off_ref[...] = off
     scaled = jnp.exp(off - jnp.max(off))
     w_ref[...] = down_lanes(scaled)
+    for b in range(FIRST, AHEAD):
+        copy_of(b).start()
 
     def exponentials(i, half, first):
         b = 2 * i + half
@@ -164,37 +174,67 @@
     emin_ref[...] = jnp.zeros_like(emin_ref)
     sweep(True)
 
-    @pl.when(jnp.max(bad_ref[...]) > 0.0)
+    low = jnp.minimum(jnp.min(tot_ref[...], axis=1, keepdims=True), TINY)
+    bad = jnp.max(bad_ref[...], axis=1, keepdims=True)
+    send_ref[...] = jnp.broadcast_to(paired(tot_ref[...])[None], send_ref.shape)
+
+    @pl.when(jnp.max(jnp.where((low < TINY) | (bad > 0.0), 1.0, 0.0)) > 0.0)
     def _():
-        sweep(False)
-
-    @pl.when(jnp.min(tot_ref[...]) < TINY)
-    def _():
-        careful(off, live_ref, e_hbm, buf, sem, None, acc_ref)
-        tot_ref[...] = rows_of(acc_ref[...])
-
-    send_ref[...] = jnp.broadcast_to(tot_ref[...][None], (N, 1, K))
+        @pl.when(jnp.max(bad_ref[...]) > 0.0)
+        def _():
+            sweep(False)
+
+        @pl.when(jnp.min(tot_ref[...]) < TINY)
+        def _():
+            careful(off, live_ref, e_hbm, buf, sem, None, acc_ref)
+            tot_ref[...] = rows_of(acc_ref[...])
+
+        send_ref[...] = jnp.broadcast_to(paired(tot_ref[...])[None], send_ref.shape)
 
 
 def second_kernel(
-    live_ref, owner_ref, slot_ref, lc_ref, off1_ref, got_ref, e_hbm, e0_ref, e1_ref, emin_ref,
-    send_ref, home_ref, off_ref, acc_ref, w_ref, ld_ref, tot_ref, buf, sem,
+    live_in, owner_in, slot_in, lc_ref, off1_ref, got_ref, e_hbm, e0_ref, e1_ref, emin_ref,
+    send_ref, home_ref, off_ref, acc_ref, w_ref, row_ref, tot_ref, buf, live_ref, owner_ref, slot_ref, sems, sem,
 ):
     halves = (e0_ref, e1_ref)
-    updated = off1_ref[...] - jnp.log(jnp.sum(got_ref[:, 0, :], axis=0, keepdims=True))
-    off = lc_ref[...] + (updated - updated[:, 0:1])
+    tables = [
+        pltpu.make_async_copy(src, dst, sems.at[i])
+        for i, (src, dst) in enumerate(((live_in, live_ref), (owner_in, owner_ref), (slot_in, slot_ref)))
+    ]
+    for table in tables:
+        table.start()
+    updated = off1_ref[...] - jnp.log(unpaired(got_ref))
+    raised = lc_ref[...] + updated
+    top = jnp.max(raised, axis=1, keepdims=True)
+    spread = top - jnp.min(raised, axis=1, keepdims=True)
+    base = updated[:, 0:1]
+    off = raised - base
     off_ref[...] = off
-    top = jnp.max(off)
-    spread = top - jnp.min(off)
-    scaled = jnp.exp(off - top)
+    level = top - base
+    scaled = jnp.exp(raised - top)
     w_ref[...] = down_lanes(scaled)
     acc_ref[...] = jnp.zeros_like(acc_ref)
+    send_ref[:, :, 0:B] = jnp.zeros((N, 1, B), jnp.float32)
+    send_ref[:, :, B + K :] = jnp.full((N, 1, G), -1.0, jnp.float32)
+    home_ref[...] = jnp.zeros_like(home_ref)
+    me = lax.axis_index(DEV)
+    for table in tables:
+        table.wait()
+
+    def place(b, row):
+        held = live_ref[b] > 0
+        here = owner_ref[b] == me
+        away = jnp.logical_and(held, jnp.logical_not(here))
+        to = jnp.where(away, owner_ref[b], me)
+        send_ref[to, :, 0:B] = row
+        send_ref[to, :, B + K :] = jnp.full((1, G), jnp.where(away, slot_ref[b], -1).astype(jnp.float32))
+        home_ref[jnp.where(jnp.logical_and(held, here), slot_ref[b], CAP)] = row
 
     def denominators(i, half):
         b = 2 * i + half
         sums = column_sums(w_ref, halves[half], i)
         live = live_lanes(live_ref, b)
-        ld_ref[b] = jnp.where(live, jnp.log(sums) + top - emin_ref[b], 0.0)
+        place(b, jnp.where(live, jnp.log(sums) + level - emin_ref[b], 0.0))
         return jnp.where(live, 1.0 / sums, 0.0)
 
     def totals(i, half, inverse):
@@ -212,31 +252,13 @@
     totals(NB // 2 - 1, 0, inverse)
     totals(NB // 2 - 1, 1, other)
     tot_ref[...] = rows_of(acc_ref[...]) * scaled
-
-    @pl.when((jnp.min(tot_ref[...]) < TINY) | (spread > SPREAD))
+    send_ref[:, :, B : B + K] = jnp.broadcast_to(tot_ref[...][None], (N, 1, K))
+    low = jnp.min(tot_ref[...], axis=1, keepdims=True)
+
+    @pl.when(jnp.max(jnp.where((low < TINY) | (spread > SPREAD), 1.0, 0.0)) > 0.0)
     def _():
-        careful(off, live_ref, e_hbm, buf, sem, ld_ref, acc_ref)
-        tot_ref[...] = rows_of(acc_ref[...])
-
-    send_ref[:, :, 0:B] = jnp.zeros((N, 1, B), jnp.float32)
-    send_ref[:, :, B : B + K] = jnp.broadcast_to(tot_ref[...][None], (N, 1, K))
-    send_ref[:, :, B + K :] = jnp.full((N, 1, G), -1.0, jnp.float32)
-    home_ref[...] = jnp.zeros_like(home_ref)
-    me = lax.axis_index(DEV)
-
-    @pl.loop(0, NB)
-    def _(b):
-        owner = owner_ref[b]
-        slot = slot_ref[b]
-
-        @pl.when((live_ref[b] > 0) & (owner == me))
-        def _():
-            home_ref[slot] = ld_ref[b]
-
-        @pl.when((live_ref[b] > 0) & (owner != me))
-        def _():
-            send_ref[owner, :, 0:B] = ld_ref[b]
-            send_ref[owner, :, B + K :] = jnp.full((1, G), slot.astype(jnp.float32))
+        careful(off, live_ref, e_hbm, buf, sem, row_ref, acc_ref, place)
+        send_ref[:, :, B : B + K] = jnp.broadcast_to(rows_of(acc_ref[...])[None], (N, 1, K))
 
 
 def third_kernel(got_ref, home_ref, off_ref, free_ref, out_ref):
@@ -252,11 +274,10 @@
         preferred_element_type=jnp.float32,
         precision=lax.Precision.HIGHEST,
     )
-    out_ref[...] = home_ref[:, 0, :] + rows[0:CAP]
+    out_ref[...] = home_ref[0:CAP, 0, :] + rows[0:CAP]
 
 
 VMEM = pl.BlockSpec(memory_space=pltpu.VMEM)
-SMEM = pl.BlockSpec(memory_space=pltpu.SMEM)
 HBM = pl.BlockSpec(memory_space=pltpu.HBM)
 
 
@@ -273,7 +294,7 @@
     half = f32(NB // 2, K, B)
     e0, e1, emin, total, log_counts, offsets = pl.pallas_call(
         first_kernel,
-        out_shape=(half, half, f32(NB, 1, B), f32(N, 1, K), f32(1, K), f32(1, K)),
+        out_shape=(half, half, f32(NB, 1, B), f32(N // 4, 8, G), f32(1, K), f32(1, K)),
         in_specs=[HBM, HBM, HBM, HBM],
         out_specs=(VMEM,) * 6,
         scratch_shapes=[
@@ -293,18 +314,22 @@
         compiler_params=params,
         name="first",
     )(live, counts, start, energies)
-    parts = lax.all_to_all(total, DEV, 0, 0, tiled=True)
+    parts = lax.all_to_all(total.reshape(N, 1, K), DEV, 0, 0, tiled=True).reshape(N // 4, 8, G)
     send, home, offsets = pl.pallas_call(
         second_kernel,
-        out_shape=(f32(N, 1, ROW), f32(CAP, 1, B), f32(1, K)),
-        in_specs=[SMEM, SMEM, SMEM, VMEM, VMEM, VMEM, HBM, VMEM, VMEM, VMEM],
+        out_shape=(f32(N, 1, ROW), f32(CAP + 1, 1, B), f32(1, K)),
+        in_specs=[VMEM, VMEM, VMEM, VMEM, VMEM, VMEM, HBM, VMEM, VMEM, VMEM],
         out_specs=(VMEM, VMEM, VMEM),
         scratch_shapes=[
             pltpu.VMEM((K, G), jnp.float32),
             pltpu.VMEM((K, G), jnp.float32),
-            pltpu.VMEM((NB, 1, B), jnp.float32),
+            pltpu.VMEM((1, 1, B), jnp.float32),
             pltpu.VMEM((1, K), jnp.float32),
             pltpu.VMEM((K, B), jnp.bfloat16),
+            pltpu.SMEM((NB,), jnp.int32),
+            pltpu.SMEM((NB,), jnp.int32),
+            pltpu.SMEM((NB,), jnp.int32),
+            pltpu.SemaphoreType.DMA((3,)),
             pltpu.SemaphoreType.DMA,
         ],
         compiler_params=params,

time: 59.7 us -> 57.7 us (0.966); the launches traced: 59.3 us -> 57.9 us
  Pallas kernels: 19.1 us -> 17.9 us
    pallas_call x2, Pallas kernels: 18.1 us -> 16.9 us  [the longest x1 12.8 us: body(): pl.pallas_call(first_kernel, out_shape=(half, half, f32(NB, 1, B), f32(N...]
where the time goes in v3:
time: 57.7 us; the launch traced here: 57.9 us
  blocking collectives  39.3 us (68%)
  Pallas kernels  17.9 us (31%)
  between operations  0.68 us (1%)
    all_to_all x1, blocking collectives, body(): lax.all_to_all(total.reshape(N, 1, K), DEV, 0, 0, tiled=True)  21.6 us
    all_to_all x1, blocking collectives, body(): got = lax.all_to_all(send, DEV, 0, 0, tiled=True)  17.8 us
    pallas_call x1, Pallas kernels, body(): pl.pallas_call(first_kernel, out_shape=(half, half, f32(NB, 1, B), f32(N...  12.8 us
    pallas_call x1, Pallas kernels, body(): pl.pallas_call(second_kernel, out_shape=(f32(N, 1, ROW), f32(CAP + 1, 1,...  4.1 us

profile of v3, /device:TPU:1, one launch (start us, length us, event | category | flops | bytes accessed | tf_op | source)
XLA Modules:
  0.0 57.9 jit_solution(10780417726989279963)
XLA Ops:
  0.6 0.0 copy-start
  0.6 0.0 copy-start.2
  0.7 0.0 copy-start.1
  0.7 12.8 %first.1 = (f32[16,256,512]{2,1,0:T(8,128)S(1)}, f32[16,256,512]{2,1,0:T(8,128)S(1)}, f32[32,1,512]{2,1,0:T(1,128)S(1)}, f32[32,8,128]{2,1,0:T(8,128)S(1)}, f32[1,256]{1,0:T(1,128)S(1)}, /*index=5*/f32[1,256]{1,0:T(1,128)S(1)}) custom-call(s32[32]{0:T(128)} %live_in.1, s32[1,256]{1,0:T(1,128)} %bitcast.7, f32[1,256]{1,0:T(1,128)} %bitcast.8, ...), custom_call_target="tpu_custom_call" | custom-call | tf_op jit(solution)/shard_map/first/pallas_call | solution.py:295
  13.5 21.6 %all_to_all.10 = f32[128,1,256]{2,1,0:T(1,128)S(1)} all-to-all(f32[128,1,256]{2,1,0:T(1,128)S(1)} %bitcast.6), channel_id=1, replica_groups=mesh['dev_0'=4,'dev_1'=4,'dev_2'=4,'dev_3'=2] {'dev_0','dev_1','dev_2','..., dimensions={0} | all-to-all | bytes 262144 | tf_op jit(solution)/shard_map/all_to_all | solution.py:317
  35.0 0.0 copy-done
  35.0 0.0 copy-done.2
  35.0 0.0 copy-done.1
  35.0 4.1 %second.1 = (f32[128,1,896]{2,1,0:T(1,128)S(1)}, f32[17,1,512]{2,1,0:T(1,128)S(1)}, f32[1,256]{1,0:T(1,128)S(1)}) custom-call(s32[32]{0:T(128)S(1)} %copy-done, s32[32]{0:T(128)S(1)} %copy-done.1, s32[32]{0:T(128)S(1)} %copy-done.2, f32[1,256]{1,0:T(1,128)S(1)} %get-tuple-element.13.lc_ref, f32[1,256]{1,0:T(1,128)S(1)} %get-tuple-element.14.off1_ref, ...), custom_call_target="tpu_custom_call" | custom-call | tf_op jit(solution)/shard_map/second/pallas_call | solution.py:318
  39.1 17.8 %all_to_all.11.got_ref = f32[128,1,896]{2,1,0:T(1,128)S(1)} all-to-all(f32[128,1,896]{2,1,0:T(1,128)S(1)} %get-tuple-element.19), channel_id=1, replica_groups=mesh['dev_0'=4,'dev_1'=4,'dev_2'=4,'dev_3'=2] {'dev_0','dev_1','dev_2','..., dimensions={0} | all-to-all | bytes 917504 | tf_op jit(solution)/shard_map/all_to_all | solution.py:338
  56.9 1.0 %third.1 = (f32[1,256]{1,0:T(1,128)}, f32[16,512]{1,0:T(8,128)}) custom-call(f32[128,1,896]{2,1,0:T(1,128)S(1)} %all_to_all.11.got_ref, f32[17,1,512]{2,1,0:T(1,128)S(1)} %get-tuple-element.20.home_ref, f32[1,256]{1,0:T(1,128)S(1)} %get-tuple-element.21.off_ref), custom_call_target="tpu_custom_call" | custom-call | tf_op jit(solution)/shard_map/third/pallas_call | solution.py:339
Async XLA Ops:
  0.6 34.4 %copy-start = (s32[32]{0:T(128)S(1)}, s32[32]{0:T(128)}, u32[]{:S(2)}) copy-start(s32[32]{0:T(128)} %live_in.1) | copy-start | bytes 388
  0.6 34.4 %copy-start.2 = (s32[32]{0:T(128)S(1)}, s32[32]{0:T(128)}, u32[]{:S(2)}) copy-start(s32[32]{0:T(128)} %slot_in.1) | copy-start | bytes 388
  0.7 34.4 %copy-start.1 = (s32[32]{0:T(128)S(1)}, s32[32]{0:T(128)}, u32[]{:S(2)}) copy-start(s32[32]{0:T(128)} %owner_in.1) | copy-start | bytes 388

commit v4 on v3

--- a/solution.py
+++ b/solution.py
@@ -10,7 +10,7 @@
 LOG2E = 1.4426950408889634
 SPREAD = 35.0
 TINY = 1e-12
-FIRST = 5
+BOUND = 17.0
 AHEAD = 8
 LARGE = 5e21
 K, B, NB, CAP, N = 256, 512, 32, 16, 128
@@ -32,7 +32,7 @@
         rows = slice(8 * c, 8 * c + 8)
         weight = w_ref[rows, :]
         for g in range(B // G):
-            term = e_ref[at, rows, g * G : (g + 1) * G] * weight
+            term = e_ref[at[0], at[1], rows, g * G : (g + 1) * G] * weight
             sums[g] = term if c == 0 else sums[g] + term
     return as_row(sums)
 
@@ -43,7 +43,7 @@
         rows = slice(8 * c, 8 * c + 8)
         part = acc_ref[rows, :]
         for g in range(B // G):
-            part = part + e_ref[at, rows, g * G : (g + 1) * G] * spread[g]
+            part = part + e_ref[at[0], at[1], rows, g * G : (g + 1) * G] * spread[g]
         acc_ref[rows, :] = part
 
 
@@ -97,7 +97,7 @@
     e0_ref, e1_ref, emin_ref, send_ref, lc_ref, off_ref,
     acc_ref, w_ref, tot_ref, bad_ref, inv_ref, raw, buf, counts, live_ref, sems, small, sem,
 ):
-    halves = (e0_ref, e1_ref)
+    turns = (e0_ref, e1_ref)
 
     def copy_of(b):
         return pltpu.make_async_copy(e_hbm.at[:, pl.ds(pl.multiple_of(b * B, B), B)], raw.at[b], sems.at[b])
@@ -109,65 +109,94 @@
     ]
     for copy in staged:
         copy.start()
-    for b in range(FIRST):
+    for b in range(AHEAD):
         copy_of(b).start()
     for copy in staged:
         copy.wait()
-    lc_ref[...] = jnp.log(counts[...].astype(jnp.float32))
+    numbers = counts[...].astype(jnp.float32)
+    scaled = numbers * jnp.exp(off_ref[...] - BOUND)
+    w_ref[...] = down_lanes(scaled)
+    lc_ref[...] = jnp.log(numbers)
     off = lc_ref[...] + off_ref[...]
     off_ref[...] = off
-    scaled = jnp.exp(off - jnp.max(off))
-    w_ref[...] = down_lanes(scaled)
-    for b in range(FIRST, AHEAD):
-        copy_of(b).start()
-
-    def exponentials(i, half, first):
-        b = 2 * i + half
-        if first:
-            copy_of(b).wait()
-
-            @pl.when(b + AHEAD < NB)
-            def _():
-                copy_of(b + AHEAD).start()
-
-        else:
-            low = jnp.min(raw[b].astype(jnp.float32), axis=0, keepdims=True)
-            emin_ref[b] = low
-            shift = jnp.broadcast_to(low, (8, B))
-        sums = [None] * (B // G)
-        for c in range(K // 8):
-            rows = slice(8 * c, 8 * c + 8)
-            weight = w_ref[rows, :]
-            for g in range(B // G):
-                energy = raw[b, rows, g * G : (g + 1) * G].astype(jnp.float32)
-                if first:
-                    value = jnp.exp2(energy * -LOG2E)
-                else:
-                    value = jnp.exp2((shift[:, g * G : (g + 1) * G] - energy) * LOG2E)
-                halves[half][i, rows, g * G : (g + 1) * G] = value
-                term = value * weight
-                sums[g] = term if c == 0 else sums[g] + term
-        total = as_row(sums)
-        bad_ref[...] = jnp.where(total <= LARGE, bad_ref[...], 1.0)
-        inv_ref[half : half + 1] = jnp.where(live_lanes(live_ref, b), 1.0 / total, 0.0)
-
-    def totals(i, half):
-        add_totals(acc_ref, halves[half], i, inv_ref[half : half + 1])
+
+    def exponentials(j, turn, first):
+        pair = 2 * j + turn
+        for h in range(2):
+            b = 2 * pair + h
+            if not first:
+                low = jnp.min(raw[b].astype(jnp.float32), axis=0, keepdims=True)
+                emin_ref[b] = low
+                shift = jnp.broadcast_to(low, (8, B))
+            sums = [None] * (B // G)
+            for c in range(K // 8):
+                rows = slice(8 * c, 8 * c + 8)
+                weight = w_ref[rows, :]
+                for g in range(B // G):
+                    energy = raw[b, rows, g * G : (g + 1) * G].astype(jnp.float32)
+                    if first:
+                        value = jnp.exp2(energy * -LOG2E)
+                    else:
+                        value = jnp.exp2((shift[:, g * G : (g + 1) * G] - energy) * LOG2E)
+                    turns[turn][j, h, rows, g * G : (g + 1) * G] = value
+                    term = value * weight
+                    sums[g] = term if c == 0 else sums[g] + term
+            total = as_row(sums)
+            bad_ref[...] = jnp.where(total <= LARGE, bad_ref[...], 1.0)
+            inv_ref[2 * turn + h] = jnp.where(live_lanes(live_ref, b), 1.0 / total, 0.0)
+
+    def totals(j, turn):
+        for h in range(2):
+            add_totals(acc_ref, turns[turn], (j, h), inv_ref[2 * turn + h])
+
+    def arrive(j, turn, more):
+        b = 2 * (2 * j + turn)
+        for h in range(2):
+            copy_of(b + h).wait()
+        if more:
+            for h in range(2):
+                copy_of(b + h + AHEAD).start()
 
     def sweep(first):
         acc_ref[...] = jnp.zeros_like(acc_ref)
+
+        def step(j, more):
+            if first:
+                arrive(j, 1, more)
+            exponentials(j, 1, first)
+            totals(j, 0)
+            if first:
+                arrive(j + 1, 0, more)
+            exponentials(j + 1, 0, first)
+            totals(j, 1)
+
+        if first:
+            arrive(0, 0, True)
         exponentials(0, 0, first)
-
-        @pl.loop(0, NB // 2 - 1)
-        def _(i):
-            exponentials(i, 1, first)
-            totals(i, 0)
-            exponentials(i + 1, 0, first)
-            totals(i, 1)
-
-        exponentials(NB // 2 - 1, 1, first)
-        totals(NB // 2 - 1, 0)
-        totals(NB // 2 - 1, 1)
+        eager = (NB - AHEAD) // 4 - 1 if first else 0
+
+        @pl.loop(0, eager)
+        def _(j):
+            step(j, True)
+
+        if first:
+            arrive(eager, 1, True)
+            exponentials(eager, 1, first)
+            totals(eager, 0)
+            arrive(eager + 1, 0, False)
+            exponentials(eager + 1, 0, first)
+            totals(eager, 1)
+
+        @pl.loop(eager + 1 if first else 0, NB // 4 - 1)
+        def _(j):
+            step(j, False)
+
+        last = NB // 4 - 1
+        if first:
+            arrive(last, 1, False)
+        exponentials(last, 1, first)
+        totals(last, 0)
+        totals(last, 1)
         tot_ref[...] = rows_of(acc_ref[...]) * scaled
 
     bad_ref[...] = jnp.zeros_like(bad_ref)
@@ -196,7 +225,7 @@
     live_in, owner_in, slot_in, lc_ref, off1_ref, got_ref, e_hbm, e0_ref, e1_ref, emin_ref,
     send_ref, home_ref, off_ref, acc_ref, w_ref, row_ref, tot_ref, buf, live_ref, owner_ref, slot_ref, sems, sem,
 ):
-    halves = (e0_ref, e1_ref)
+    turns = (e0_ref, e1_ref)
     tables = [
         pltpu.make_async_copy(src, dst, sems.at[i])
         for i, (src, dst) in enumerate(((live_in, live_ref), (owner_in, owner_ref), (slot_in, slot_ref)))
@@ -218,8 +247,6 @@
     send_ref[:, :, B + K :] = jnp.full((N, 1, G), -1.0, jnp.float32)
     home_ref[...] = jnp.zeros_like(home_ref)
     me = lax.axis_index(DEV)
-    for table in tables:
-        table.wait()
 
     def place(b, row):
         held = live_ref[b] > 0
@@ -230,27 +257,34 @@
         send_ref[to, :, B + K :] = jnp.full((1, G), jnp.where(away, slot_ref[b], -1).astype(jnp.float32))
         home_ref[jnp.where(jnp.logical_and(held, here), slot_ref[b], CAP)] = row
 
-    def denominators(i, half):
-        b = 2 * i + half
-        sums = column_sums(w_ref, halves[half], i)
+    def settle(b, sums):
         live = live_lanes(live_ref, b)
         place(b, jnp.where(live, jnp.log(sums) + level - emin_ref[b], 0.0))
         return jnp.where(live, 1.0 / sums, 0.0)
 
-    def totals(i, half, inverse):
-        add_totals(acc_ref, halves[half], i, inverse)
-
-    def body(i, inverse):
-        other = denominators(i, 1)
-        totals(i, 0, inverse)
-        inverse = denominators(i + 1, 0)
-        totals(i, 1, other)
-        return inverse
-
-    inverse = lax.fori_loop(0, NB // 2 - 1, body, denominators(0, 0))
-    other = denominators(NB // 2 - 1, 1)
-    totals(NB // 2 - 1, 0, inverse)
-    totals(NB // 2 - 1, 1, other)
+    def denominators(j, turn):
+        sums = [column_sums(w_ref, turns[turn], (j, h)) for h in range(2)]
+        return [settle(4 * j + 2 * turn + h, sums[h]) for h in range(2)]
+
+    def totals(j, turn, inverses):
+        for h in range(2):
+            add_totals(acc_ref, turns[turn], (j, h), inverses[h])
+
+    def body(j, inverses):
+        others = denominators(j, 1)
+        totals(j, 0, inverses)
+        inverses = denominators(j + 1, 0)
+        totals(j, 1, others)
+        return inverses
+
+    sums = [column_sums(w_ref, e0_ref, (0, h)) for h in range(2)]
+    for table in tables:
+        table.wait()
+    last = NB // 4 - 1
+    inverses = lax.fori_loop(0, last, body, [settle(h, sums[h]) for h in range(2)])
+    others = denominators(last, 1)
+    totals(last, 0, inverses)
+    totals(last, 1, others)
     tot_ref[...] = rows_of(acc_ref[...]) * scaled
     send_ref[:, :, B : B + K] = jnp.broadcast_to(tot_ref[...][None], (N, 1, K))
     low = jnp.min(tot_ref[...], axis=1, keepdims=True)
@@ -262,14 +296,14 @@
 
 
 def third_kernel(got_ref, home_ref, off_ref, free_ref, out_ref):
-    total = jnp.sum(got_ref[:, 0, B : B + K], axis=0, keepdims=True)
+    words = [got_ref[pl.ds(j, N, stride=ROW // G), :] for j in range(ROW // G)]
+    total = jnp.concatenate([jnp.sum(word, axis=0, keepdims=True) for word in words[4:6]], axis=1)
     updated = off_ref[...] - jnp.log(total)
     free_ref[...] = updated - updated[:, 0:1]
     lane = lax.broadcasted_iota(jnp.int32, (N, G), 1).astype(jnp.float32)
-    chosen = jnp.where(got_ref[:, 0, B + K :] == lane, 1.0, 0.0)
     rows = lax.dot_general(
-        chosen,
-        got_ref[:, 0, 0:B],
+        jnp.where(words[6] == lane, 1.0, 0.0),
+        jnp.concatenate(words[0:4], axis=1),
         (((0,), (0,)), ((), ())),
         preferred_element_type=jnp.float32,
         precision=lax.Precision.HIGHEST,
@@ -291,7 +325,7 @@
         pltpu.with_memory_space_constraint(value, pltpu.HBM)
         for value in (energies, block_live_samples, state_counts[None], start_free[None])
     )
-    half = f32(NB // 2, K, B)
+    half = f32(NB // 4, 2, K, B)
     e0, e1, emin, total, log_counts, offsets = pl.pallas_call(
         first_kernel,
         out_shape=(half, half, f32(NB, 1, B), f32(N // 4, 8, G), f32(1, K), f32(1, K)),
@@ -302,7 +336,7 @@
             pltpu.VMEM((K, G), jnp.float32),
             pltpu.VMEM((1, K), jnp.float32),
             pltpu.VMEM((1, B), jnp.float32),
-            pltpu.VMEM((2, B), jnp.float32),
+            pltpu.VMEM((4, 1, B), jnp.float32),
             pltpu.VMEM((NB, K, B), jnp.bfloat16),
             pltpu.VMEM((K, B), jnp.bfloat16),
             pltpu.VMEM((1, K), jnp.int32),
@@ -335,7 +369,7 @@
         compiler_params=params,
         name="second",
     )(block_live_samples, block_owner, block_slot, log_counts, offsets, parts, energies, e0, e1, emin)
-    got = lax.all_to_all(send, DEV, 0, 0, tiled=True)
+    got = lax.all_to_all(send, DEV, 0, 0, tiled=True).reshape(N * ROW // G, G)
     free, placed = pl.pallas_call(
         third_kernel,
         out_shape=(f32(1, K), f32(CAP, B)),

time: 57.7 us -> 56.9 us (0.986)
  blocking collectives: 39.3 us -> 38.5 us
    all_to_all x1, blocking collectives: 17.8 us -> 17.1 us  [body(): got = lax.all_to_all(send, DEV, 0, 0, tiled=True).reshape(N * ROW // G, G)]
where the time goes in v4:
time: 56.9 us; the launch traced here: 56.6 us
  blocking collectives  38.5 us (68%)
  Pallas kernels  17.4 us (31%)
  between operations  0.68 us (1%)
    all_to_all x1, blocking collectives, body(): lax.all_to_all(total.reshape(N, 1, K), DEV, 0, 0, tiled=True)  21.3 us
    all_to_all x1, blocking collectives, body(): got = lax.all_to_all(send, DEV, 0, 0, tiled=True).reshape(N * ROW // G, G)  17.1 us
    pallas_call x1, Pallas kernels, body(): pl.pallas_call(first_kernel, out_shape=(half, half, f32(NB, 1, B), f32(N...  12.9 us
    pallas_call x1, Pallas kernels, body(): pl.pallas_call(second_kernel, out_shape=(f32(N, 1, ROW), f32(CAP + 1, 1,...  3.56 us

profile of v4, /device:TPU:1, one launch (start us, length us, event | category | flops | bytes accessed | tf_op | source)
XLA Modules:
  0.0 56.6 jit_solution(1256075929471350243)
XLA Ops:
  0.6 0.0 copy-start
  0.6 0.0 copy-start.2
  0.7 0.0 copy-start.1
  0.7 12.9 %first.1 = (f32[8,2,256,512]{3,2,1,0:T(8,128)S(1)}, f32[8,2,256,512]{3,2,1,0:T(8,128)S(1)}, f32[32,1,512]{2,1,0:T(1,128)S(1)}, f32[32,8,128]{2,1,0:T(8,128)S(1)}...) custom-call(s32[32]{0:T(128)} %live_in.1, s32[1,256]{1,0:T(1,128)} %bitcast.9, f32[1,256]{1,0:T(1,128)} %bitcast.10, ...), custom_call_target="tpu_custom_call" | custom-call | tf_op jit(solution)/shard_map/first/pallas_call | solution.py:329
  13.5 21.3 %all_to_all.10 = f32[128,1,256]{2,1,0:T(1,128)S(1)} all-to-all(f32[128,1,256]{2,1,0:T(1,128)S(1)} %bitcast.8), channel_id=1, replica_groups=mesh['dev_0'=4,'dev_1'=4,'dev_2'=4,'dev_3'=2] {'dev_0','dev_1','dev_2','..., dimensions={0} | all-to-all | bytes 262144 | tf_op jit(solution)/shard_map/all_to_all | solution.py:351
  34.9 0.0 copy-done
  34.9 0.0 copy-done.2
  34.9 0.0 copy-done.1
  34.9 3.6 %second.1 = (f32[128,1,896]{2,1,0:T(1,128)S(1)}, f32[17,1,512]{2,1,0:T(1,128)S(1)}, f32[1,256]{1,0:T(1,128)S(1)}) custom-call(s32[32]{0:T(128)S(1)} %copy-done, s32[32]{0:T(128)S(1)} %copy-done.1, s32[32]{0:T(128)S(1)} %copy-done.2, f32[1,256]{1,0:T(1,128)S(1)} %get-tuple-element.13.lc_ref, f32[1,256]{1,0:T(1,128)S(1)} %get-tuple-element.14.off1_ref, ...), custom_call_target="tpu_custom_call" | custom-call | tf_op jit(solution)/shard_map/second/pallas_call | solution.py:352
  38.5 17.1 %all_to_all.11 = f32[128,1,896]{2,1,0:T(1,128)S(1)} all-to-all(f32[128,1,896]{2,1,0:T(1,128)S(1)} %get-tuple-element.19), channel_id=1, replica_groups=mesh['dev_0'=4,'dev_1'=4,'dev_2'=4,'dev_3'=2] {'dev_0','dev_1','dev_2','..., dimensions={0} | all-to-all | bytes 917504 | tf_op jit(solution)/shard_map/all_to_all | solution.py:372
  55.6 1.0 %third.1 = (f32[1,256]{1,0:T(1,128)}, f32[16,512]{1,0:T(8,128)}) custom-call(f32[896,128]{1,0:T(8,128)S(1)} %bitcast.6, f32[17,1,512]{2,1,0:T(1,128)S(1)} %get-tuple-element.20.home_ref, f32[1,256]{1,0:T(1,128)S(1)} %get-tuple-element.21.off_ref), custom_call_target="tpu_custom_call" | custom-call | tf_op jit(solution)/shard_map/third/pallas_call | solution.py:373
Async XLA Ops:
  0.6 34.2 %copy-start = (s32[32]{0:T(128)S(1)}, s32[32]{0:T(128)}, u32[]{:S(2)}) copy-start(s32[32]{0:T(128)} %live_in.1) | copy-start | bytes 388
  0.6 34.2 %copy-start.2 = (s32[32]{0:T(128)S(1)}, s32[32]{0:T(128)}, u32[]{:S(2)}) copy-start(s32[32]{0:T(128)} %slot_in.1) | copy-start | bytes 388
  0.7 34.2 %copy-start.1 = (s32[32]{0:T(128)S(1)}, s32[32]{0:T(128)}, u32[]{:S(2)}) copy-start(s32[32]{0:T(128)} %owner_in.1) | copy-start | bytes 388

commit v5 on v4

--- a/solution.py
+++ b/solution.py
@@ -65,6 +65,13 @@
 
 def live_lanes(live_ref, b):
     return lax.broadcasted_iota(jnp.int32, (1, B), 1) < live_ref[b]
+
+
+def samples(live_ref):
+    total = live_ref[0]
+    for b in range(1, NB):
+        total = total + live_ref[b]
+    return total
 
 
 def careful(off, live_ref, e_hbm, buf, sem, ld_ref, acc_ref, place=None):
@@ -119,6 +126,7 @@
     lc_ref[...] = jnp.log(numbers)
     off = lc_ref[...] + off_ref[...]
     off_ref[...] = off
+    held = jnp.where(samples(live_ref) > 0, TINY, -1.0)
 
     def exponentials(j, turn, first):
         pair = 2 * j + turn
@@ -203,17 +211,17 @@
     emin_ref[...] = jnp.zeros_like(emin_ref)
     sweep(True)
 
-    low = jnp.minimum(jnp.min(tot_ref[...], axis=1, keepdims=True), TINY)
+    low = jnp.min(tot_ref[...], axis=1, keepdims=True)
     bad = jnp.max(bad_ref[...], axis=1, keepdims=True)
     send_ref[...] = jnp.broadcast_to(paired(tot_ref[...])[None], send_ref.shape)
 
-    @pl.when(jnp.max(jnp.where((low < TINY) | (bad > 0.0), 1.0, 0.0)) > 0.0)
+    @pl.when(jnp.max(jnp.where((low < held) | (bad > 0.0), 1.0, 0.0)) > 0.0)
     def _():
         @pl.when(jnp.max(bad_ref[...]) > 0.0)
         def _():
             sweep(False)
 
-        @pl.when(jnp.min(tot_ref[...]) < TINY)
+        @pl.when(jnp.min(tot_ref[...]) < held)
         def _():
             careful(off, live_ref, e_hbm, buf, sem, None, acc_ref)
             tot_ref[...] = rows_of(acc_ref[...])
@@ -280,6 +288,7 @@
     sums = [column_sums(w_ref, e0_ref, (0, h)) for h in range(2)]
     for table in tables:
         table.wait()
+    held = jnp.where(samples(live_ref) > 0, TINY, -1.0)
     last = NB // 4 - 1
     inverses = lax.fori_loop(0, last, body, [settle(h, sums[h]) for h in range(2)])
     others = denominators(last, 1)
@@ -289,7 +298,7 @@
     send_ref[:, :, B : B + K] = jnp.broadcast_to(tot_ref[...][None], (N, 1, K))
     low = jnp.min(tot_ref[...], axis=1, keepdims=True)
 
-    @pl.when(jnp.max(jnp.where((low < TINY) | (spread > SPREAD), 1.0, 0.0)) > 0.0)
+    @pl.when(jnp.max(jnp.where((low < held) | ((spread > SPREAD) & (held > 0.0)), 1.0, 0.0)) > 0.0)
     def _():
         careful(off, live_ref, e_hbm, buf, sem, row_ref, acc_ref, place)
         send_ref[:, :, B : B + K] = jnp.broadcast_to(rows_of(acc_ref[...])[None], (N, 1, K))

time: 56.9 us -> 56.8 us (level)
  no operation moved by 1% of the time
where the time goes in v5:
time: 56.8 us; the launch traced here: 56.6 us
  blocking collectives  38.5 us (68%)
  Pallas kernels  17.4 us (31%)
  between operations  0.68 us (1%)
    all_to_all x1, blocking collectives, body(): lax.all_to_all(total.reshape(N, 1, K), DEV, 0, 0, tiled=True)  21.3 us
    all_to_all x1, blocking collectives, body(): got = lax.all_to_all(send, DEV, 0, 0, tiled=True).reshape(N * ROW // G, G)  17.1 us
    pallas_call x1, Pallas kernels, body(): pl.pallas_call(first_kernel, out_shape=(half, half, f32(NB, 1, B), f32(N...  12.9 us
    pallas_call x1, Pallas kernels, body(): pl.pallas_call(second_kernel, out_shape=(f32(N, 1, ROW), f32(CAP + 1, 1,...  3.56 us

profile of v5, /device:TPU:1, one launch (start us, length us, event | category | flops | bytes accessed | tf_op | source)
XLA Modules:
  0.0 56.6 jit_solution(12857988877409939736)
XLA Ops:
  0.6 0.0 copy-start
  0.6 0.0 copy-start.2
  0.7 0.0 copy-start.1
  0.7 12.9 %first.1 = (f32[8,2,256,512]{3,2,1,0:T(8,128)S(1)}, f32[8,2,256,512]{3,2,1,0:T(8,128)S(1)}, f32[32,1,512]{2,1,0:T(1,128)S(1)}, f32[32,8,128]{2,1,0:T(8,128)S(1)}...) custom-call(s32[32]{0:T(128)} %live_in.1, s32[1,256]{1,0:T(1,128)} %bitcast.9, f32[1,256]{1,0:T(1,128)} %bitcast.10, ...), custom_call_target="tpu_custom_call" | custom-call | tf_op jit(solution)/shard_map/first/pallas_call | solution.py:338
  13.5 21.3 %all_to_all.10 = f32[128,1,256]{2,1,0:T(1,128)S(1)} all-to-all(f32[128,1,256]{2,1,0:T(1,128)S(1)} %bitcast.8), channel_id=1, replica_groups=mesh['dev_0'=4,'dev_1'=4,'dev_2'=4,'dev_3'=2] {'dev_0','dev_1','dev_2','..., dimensions={0} | all-to-all | bytes 262144 | tf_op jit(solution)/shard_map/all_to_all | solution.py:360
  34.9 0.0 copy-done
  34.9 0.0 copy-done.2
  34.9 0.0 copy-done.1
  34.9 3.6 %second.1 = (f32[128,1,896]{2,1,0:T(1,128)S(1)}, f32[17,1,512]{2,1,0:T(1,128)S(1)}, f32[1,256]{1,0:T(1,128)S(1)}) custom-call(s32[32]{0:T(128)S(1)} %copy-done, s32[32]{0:T(128)S(1)} %copy-done.1, s32[32]{0:T(128)S(1)} %copy-done.2, f32[1,256]{1,0:T(1,128)S(1)} %get-tuple-element.13.lc_ref, f32[1,256]{1,0:T(1,128)S(1)} %get-tuple-element.14.off1_ref, ...), custom_call_target="tpu_custom_call" | custom-call | tf_op jit(solution)/shard_map/second/pallas_call | solution.py:361
  38.5 17.1 %all_to_all.11 = f32[128,1,896]{2,1,0:T(1,128)S(1)} all-to-all(f32[128,1,896]{2,1,0:T(1,128)S(1)} %get-tuple-element.19), channel_id=1, replica_groups=mesh['dev_0'=4,'dev_1'=4,'dev_2'=4,'dev_3'=2] {'dev_0','dev_1','dev_2','..., dimensions={0} | all-to-all | bytes 917504 | tf_op jit(solution)/shard_map/all_to_all | solution.py:381
  55.6 1.0 %third.1 = (f32[1,256]{1,0:T(1,128)}, f32[16,512]{1,0:T(8,128)}) custom-call(f32[896,128]{1,0:T(8,128)S(1)} %bitcast.6, f32[17,1,512]{2,1,0:T(1,128)S(1)} %get-tuple-element.20.home_ref, f32[1,256]{1,0:T(1,128)S(1)} %get-tuple-element.21.off_ref), custom_call_target="tpu_custom_call" | custom-call | tf_op jit(solution)/shard_map/third/pallas_call | solution.py:382
Async XLA Ops:
  0.6 34.2 %copy-start = (s32[32]{0:T(128)S(1)}, s32[32]{0:T(128)}, u32[]{:S(2)}) copy-start(s32[32]{0:T(128)} %live_in.1) | copy-start | bytes 388
  0.6 34.2 %copy-start.2 = (s32[32]{0:T(128)S(1)}, s32[32]{0:T(128)}, u32[]{:S(2)}) copy-start(s32[32]{0:T(128)} %slot_in.1) | copy-start | bytes 388
  0.7 34.2 %copy-start.1 = (s32[32]{0:T(128)S(1)}, s32[32]{0:T(128)}, u32[]{:S(2)}) copy-start(s32[32]{0:T(128)} %owner_in.1) | copy-start | bytes 388

commit v6 on v5

--- a/solution.py
+++ b/solution.py
@@ -65,6 +65,21 @@
 
 def live_lanes(live_ref, b):
     return lax.broadcasted_iota(jnp.int32, (1, B), 1) < live_ref[b]
+
+
+def arrange(live_ref, from_ref, fill_ref):
+    for b in range(AHEAD):
+        from_ref[b] = b
+        fill_ref[b] = live_ref[b]
+    taken = jnp.int32(AHEAD)
+    for b in range(AHEAD, NB):
+        from_ref[taken] = b
+        fill_ref[taken] = live_ref[b]
+        taken = taken + jnp.where(live_ref[b] > 0, 1, 0)
+    for more in range(4):
+        from_ref[taken + more] = 0
+        fill_ref[taken + more] = 0
+    return (taken + 3) // 4
 
 
 def samples(live_ref):
@@ -96,18 +111,18 @@
                     ld_ref[0, :, lanes] = jnp.where(live, log_denom, 0.0)
                 acc_ref[...] += jnp.where(live, jnp.exp(shifted - log_denom), 0.0)
             if place is not None:
-                place(b, ld_ref[0])
+                place(b, True, ld_ref[0])
 
 
 def first_kernel(
     live_hbm, counts_hbm, free_hbm, e_hbm,
     e0_ref, e1_ref, emin_ref, send_ref, lc_ref, off_ref,
-    acc_ref, w_ref, tot_ref, bad_ref, inv_ref, raw, buf, counts, live_ref, sems, small, sem,
+    acc_ref, w_ref, tot_ref, bad_ref, inv_ref, raw, buf, counts, live_ref, from_ref, fill_ref, sems, small, sem,
 ):
     turns = (e0_ref, e1_ref)
 
-    def copy_of(b):
-        return pltpu.make_async_copy(e_hbm.at[:, pl.ds(pl.multiple_of(b * B, B), B)], raw.at[b], sems.at[b])
+    def copy_of(q, b):
+        return pltpu.make_async_copy(e_hbm.at[:, pl.ds(pl.multiple_of(b * B, B), B)], raw.at[q], sems.at[q])
 
     staged = [
         pltpu.make_async_copy(counts_hbm, counts, small.at[0]),
@@ -117,7 +132,7 @@
     for copy in staged:
         copy.start()
     for b in range(AHEAD):
-        copy_of(b).start()
+        copy_of(b, b).start()
     for copy in staged:
         copy.wait()
     numbers = counts[...].astype(jnp.float32)
@@ -127,6 +142,7 @@
     off = lc_ref[...] + off_ref[...]
     off_ref[...] = off
     held = jnp.where(samples(live_ref) > 0, TINY, -1.0)
+    fours = arrange(live_ref, from_ref, fill_ref)
 
     def exponentials(j, turn, first):
         pair = 2 * j + turn
@@ -151,57 +167,42 @@
                     sums[g] = term if c == 0 else sums[g] + term
             total = as_row(sums)
             bad_ref[...] = jnp.where(total <= LARGE, bad_ref[...], 1.0)
-            inv_ref[2 * turn + h] = jnp.where(live_lanes(live_ref, b), 1.0 / total, 0.0)
+            inv_ref[2 * turn + h] = jnp.where(live_lanes(fill_ref, b), 1.0 / total, 0.0)
 
     def totals(j, turn):
         for h in range(2):
             add_totals(acc_ref, turns[turn], (j, h), inv_ref[2 * turn + h])
 
-    def arrive(j, turn, more):
-        b = 2 * (2 * j + turn)
+    def arrive(j, turn):
+        q = 2 * (2 * j + turn)
         for h in range(2):
-            copy_of(b + h).wait()
-        if more:
+            copy_of(q + h, from_ref[q + h]).wait()
+
+        @pl.when(q + AHEAD < 4 * fours)
+        def _():
             for h in range(2):
-                copy_of(b + h + AHEAD).start()
+                copy_of(q + h + AHEAD, from_ref[q + h + AHEAD]).start()
 
     def sweep(first):
         acc_ref[...] = jnp.zeros_like(acc_ref)
-
-        def step(j, more):
+        if first:
+            arrive(0, 0)
+        exponentials(0, 0, first)
+        last = fours - 1
+
+        @pl.loop(0, last)
+        def _(j):
             if first:
-                arrive(j, 1, more)
+                arrive(j, 1)
             exponentials(j, 1, first)
             totals(j, 0)
             if first:
-                arrive(j + 1, 0, more)
+                arrive(j + 1, 0)
             exponentials(j + 1, 0, first)
             totals(j, 1)
 
         if first:
-            arrive(0, 0, True)
-        exponentials(0, 0, first)
-        eager = (NB - AHEAD) // 4 - 1 if first else 0
-
-        @pl.loop(0, eager)
-        def _(j):
-            step(j, True)
-
-        if first:
-            arrive(eager, 1, True)
-            exponentials(eager, 1, first)
-            totals(eager, 0)
-            arrive(eager + 1, 0, False)
-            exponentials(eager + 1, 0, first)
-            totals(eager, 1)
-
-        @pl.loop(eager + 1 if first else 0, NB // 4 - 1)
-        def _(j):
-            step(j, False)
-
-        last = NB // 4 - 1
-        if first:
-            arrive(last, 1, False)
+            arrive(last, 1)
         exponentials(last, 1, first)
         totals(last, 0)
         totals(last, 1)
@@ -231,7 +232,7 @@
 
 def second_kernel(
     live_in, owner_in, slot_in, lc_ref, off1_ref, got_ref, e_hbm, e0_ref, e1_ref, emin_ref,
-    send_ref, home_ref, off_ref, acc_ref, w_ref, row_ref, tot_ref, buf, live_ref, owner_ref, slot_ref, sems, sem,
+    send_ref, home_ref, off_ref, acc_ref, w_ref, row_ref, tot_ref, buf, live_ref, owner_ref, slot_ref, from_ref, fill_ref, sems, sem,
 ):
     turns = (e0_ref, e1_ref)
     tables = [
@@ -256,8 +257,7 @@
     home_ref[...] = jnp.zeros_like(home_ref)
     me = lax.axis_index(DEV)
 
-    def place(b, row):
-        held = live_ref[b] > 0
+    def place(b, held, row):
         here = owner_ref[b] == me
         away = jnp.logical_and(held, jnp.logical_not(here))
         to = jnp.where(away, owner_ref[b], me)
@@ -265,9 +265,9 @@
         send_ref[to, :, B + K :] = jnp.full((1, G), jnp.where(away, slot_ref[b], -1).astype(jnp.float32))
         home_ref[jnp.where(jnp.logical_and(held, here), slot_ref[b], CAP)] = row
 
-    def settle(b, sums):
-        live = live_lanes(live_ref, b)
-        place(b, jnp.where(live, jnp.log(sums) + level - emin_ref[b], 0.0))
+    def settle(q, sums):
+        live = live_lanes(fill_ref, q)
+        place(from_ref[q], fill_ref[q] > 0, jnp.where(live, jnp.log(sums) + level - emin_ref[q], 0.0))
         return jnp.where(live, 1.0 / sums, 0.0)
 
     def denominators(j, turn):
@@ -289,7 +289,7 @@
     for table in tables:
         table.wait()
     held = jnp.where(samples(live_ref) > 0, TINY, -1.0)
-    last = NB // 4 - 1
+    last = arrange(live_ref, from_ref, fill_ref) - 1
     inverses = lax.fori_loop(0, last, body, [settle(h, sums[h]) for h in range(2)])
     others = denominators(last, 1)
     totals(last, 0, inverses)
@@ -350,6 +350,8 @@
             pltpu.VMEM((K, B), jnp.bfloat16),
             pltpu.VMEM((1, K), jnp.int32),
             pltpu.SMEM((NB,), jnp.int32),
+            pltpu.SMEM((NB + 8,), jnp.int32),
+            pltpu.SMEM((NB + 8,), jnp.int32),
             pltpu.SemaphoreType.DMA((NB,)),
             pltpu.SemaphoreType.DMA((3,)),
             pltpu.SemaphoreType.DMA,
@@ -372,6 +374,8 @@
             pltpu.SMEM((NB,), jnp.int32),
             pltpu.SMEM((NB,), jnp.int32),
             pltpu.SMEM((NB,), jnp.int32),
+            pltpu.SMEM((NB + 8,), jnp.int32),
+            pltpu.SMEM((NB + 8,), jnp.int32),
             pltpu.SemaphoreType.DMA((3,)),
             pltpu.SemaphoreType.DMA,
         ],

time: 56.8 us -> 56.3 us (level)
  Pallas kernels: 17.4 us -> 7.51 us
  blocking collectives: 38.5 us -> 47.6 us
    pallas_call x1, Pallas kernels: 12.9 us -> 4.92 us  [body(): pl.pallas_call(first_kernel, out_shape=(half, half, f32(NB, 1, B), f32(N...]
    all_to_all x1, blocking collectives: 21.3 us -> 28.8 us  [body(): lax.all_to_all(total.reshape(N, 1, K), DEV, 0, 0, tiled=True)]
    pallas_call x1, Pallas kernels: 3.56 us -> 1.58 us  [body(): pl.pallas_call(second_kernel, out_shape=(f32(N, 1, ROW), f32(CAP + 1, 1,...]
    all_to_all x1, blocking collectives: 17.1 us -> 18.8 us  [body(): got = lax.all_to_all(send, DEV, 0, 0, tiled=True).reshape(N * ROW // G, G)]
where the time goes in v6:
time: 56.3 us; the launch traced here: 55.8 us
  blocking collectives  47.6 us (85%)
  Pallas kernels  7.51 us (13%)
  between operations  0.68 us (1%)
    all_to_all x1, blocking collectives, body(): lax.all_to_all(total.reshape(N, 1, K), DEV, 0, 0, tiled=True)  28.8 us
    all_to_all x1, blocking collectives, body(): got = lax.all_to_all(send, DEV, 0, 0, tiled=True).reshape(N * ROW // G, G)  18.8 us
    pallas_call x1, Pallas kernels, body(): pl.pallas_call(first_kernel, out_shape=(half, half, f32(NB, 1, B), f32(N...  4.92 us
    pallas_call x1, Pallas kernels, body(): pl.pallas_call(second_kernel, out_shape=(f32(N, 1, ROW), f32(CAP + 1, 1,...  1.58 us

profile of v6, /device:TPU:1, one launch (start us, length us, event | category | flops | bytes accessed | tf_op | source)
XLA Modules:
  0.0 55.8 jit_solution(15995506418150623837)
XLA Ops:
  0.6 0.0 copy-start
  0.6 0.0 copy-start.2
  0.7 0.0 copy-start.1
  0.7 4.9 %first.1 = (f32[8,2,256,512]{3,2,1,0:T(8,128)S(1)}, f32[8,2,256,512]{3,2,1,0:T(8,128)S(1)}, f32[32,1,512]{2,1,0:T(1,128)S(1)}, f32[32,8,128]{2,1,0:T(8,128)S(1)}...) custom-call(s32[32]{0:T(128)} %live_in.1, s32[1,256]{1,0:T(1,128)} %bitcast.9, f32[1,256]{1,0:T(1,128)} %bitcast.10, ...), custom_call_target="tpu_custom_call" | custom-call | tf_op jit(solution)/shard_map/first/pallas_call | solution.py:338
  5.6 28.8 %all_to_all.10 = f32[128,1,256]{2,1,0:T(1,128)S(1)} all-to-all(f32[128,1,256]{2,1,0:T(1,128)S(1)} %bitcast.8), channel_id=1, replica_groups=mesh['dev_0'=4,'dev_1'=4,'dev_2'=4,'dev_3'=2] {'dev_0','dev_1','dev_2','..., dimensions={0} | all-to-all | bytes 262144 | tf_op jit(solution)/shard_map/all_to_all | solution.py:362
  34.4 0.0 copy-done
  34.4 0.0 copy-done.2
  34.4 0.0 copy-done.1
  34.4 1.6 %second.1 = (f32[128,1,896]{2,1,0:T(1,128)S(1)}, f32[17,1,512]{2,1,0:T(1,128)S(1)}, f32[1,256]{1,0:T(1,128)S(1)}) custom-call(s32[32]{0:T(128)S(1)} %copy-done, s32[32]{0:T(128)S(1)} %copy-done.1, s32[32]{0:T(128)S(1)} %copy-done.2, f32[1,256]{1,0:T(1,128)S(1)} %get-tuple-element.13.lc_ref, f32[1,256]{1,0:T(1,128)S(1)} %get-tuple-element.14.off1_ref, ...), custom_call_target="tpu_custom_call" | custom-call | tf_op jit(solution)/shard_map/second/pallas_call | solution.py:363
  36.0 18.8 %all_to_all.11 = f32[128,1,896]{2,1,0:T(1,128)S(1)} all-to-all(f32[128,1,896]{2,1,0:T(1,128)S(1)} %get-tuple-element.19), channel_id=1, replica_groups=mesh['dev_0'=4,'dev_1'=4,'dev_2'=4,'dev_3'=2] {'dev_0','dev_1','dev_2','..., dimensions={0} | all-to-all | bytes 917504 | tf_op jit(solution)/shard_map/all_to_all | solution.py:385
  54.8 1.0 %third.1 = (f32[1,256]{1,0:T(1,128)}, f32[16,512]{1,0:T(8,128)}) custom-call(f32[896,128]{1,0:T(8,128)S(1)} %bitcast.6, f32[17,1,512]{2,1,0:T(1,128)S(1)} %get-tuple-element.20.home_ref, f32[1,256]{1,0:T(1,128)S(1)} %get-tuple-element.21.off_ref), custom_call_target="tpu_custom_call" | custom-call | tf_op jit(solution)/shard_map/third/pallas_call | solution.py:386
Async XLA Ops:
  0.6 33.8 %copy-start = (s32[32]{0:T(128)S(1)}, s32[32]{0:T(128)}, u32[]{:S(2)}) copy-start(s32[32]{0:T(128)} %live_in.1) | copy-start | bytes 388
  0.6 33.7 %copy-start.2 = (s32[32]{0:T(128)S(1)}, s32[32]{0:T(128)}, u32[]{:S(2)}) copy-start(s32[32]{0:T(128)} %slot_in.1) | copy-start | bytes 388
  0.7 33.7 %copy-start.1 = (s32[32]{0:T(128)S(1)}, s32[32]{0:T(128)}, u32[]{:S(2)}) copy-start(s32[32]{0:T(128)} %owner_in.1) | copy-start | bytes 388
